TPU v7x, 128 devices: a whole 4x4x4 slice. The times are simulated.
128 devices in a mesh: fsdp: 16 (over x, y), seq: 8 (over z, core).
Axes of the slice: x: 4, y: 4, z: 4, core: 2. Of those that a mesh axis runs over, the one named last changes fastest.
Arguments:
- tokens: bfloat16 [16, 4096, 4096], P('fsdp', 'seq'), may hold values from -72 to 72
- norm_gain: float32 [4096], replicated, may hold values from 0.1 to 1.9
- lru_proj: bfloat16 [4096, 2048], P(('fsdp', 'seq')), may hold values from -0.09375 to 0.09375
- gelu_proj: bfloat16 [4096, 2048], P(('fsdp', 'seq')), may hold values from -0.09375 to 0.09375
- conv_weight: float32 [4, 2048], replicated, may hold values from -3 to 3
- conv_bias: float32 [2048], replicated, may hold values from -3 to 3
- gate_weights: bfloat16 [2048, 512], P('seq'), may hold values from -0.375 to 0.375
- gate_bias: float32 [2, 2048], replicated, may hold values from -4 to 4
- decay_param: float32 [2048], replicated, may hold values from -13 to -2
Outputs:
- recurrent_out: bfloat16 [16, 4096, 2048], P('fsdp', 'seq')
All inputs are finite; a program needn't handle non-finite values.
Results may differ from a plain program's by a relative error of at most 0.0051.
Values may be sent and summed in bfloat16 or wider, within the bound.
A program may use at most 128 MiB of HBM per device.

v0:
```python
import jax
import jax.numpy as jnp
from jax import lax
from jax.sharding import PartitionSpec as P


def from_behind(x, axis, by):
    devices = lax.axis_size(axis)
    pairs = [(i, i + by) for i in range(devices) if 0 <= i + by < devices]
    return lax.ppermute(x, axis, pairs)


def block_scan(decay, driven):
    seq_count, tok_rows, inner = decay.shape
    block_rows = tok_rows
    for candidate in (64, 32, 16, 8):
        block_rows = candidate
        break
    block_count = tok_rows // block_rows
    decay_blocks = decay.reshape(seq_count, block_count, block_rows, inner)
    driven_blocks = driven.reshape(seq_count, block_count, block_rows, inner)
    running_decay = decay_blocks[:, :, 0]
    running_state = driven_blocks[:, :, 0]
    decay_list = [running_decay]
    state_list = [running_state]
    for offset in range(1, block_rows):
        decay_now = decay_blocks[:, :, offset]
        running_decay = running_decay * decay_now
        running_state = decay_now * running_state + driven_blocks[:, :, offset]
        decay_list.append(running_decay)
        state_list.append(running_state)
    within_decay = jnp.stack(decay_list, axis=2)
    within_state = jnp.stack(state_list, axis=2)
    carry_state = jnp.zeros((seq_count, inner), jnp.float32)
    carry_decay = jnp.ones((seq_count, inner), jnp.float32)
    start_list = []
    prefix_list = []
    for block_index in range(block_count):
        start_list.append(carry_state)
        prefix_list.append(carry_decay)
        carry_state = running_decay[:, block_index] * carry_state + running_state[:, block_index]
        carry_decay = carry_decay * running_decay[:, block_index]
    block_start = jnp.stack(start_list, axis=1)
    block_prefix = jnp.stack(prefix_list, axis=1)
    cumulative = (within_decay * block_prefix[:, :, None, :]).reshape(seq_count, tok_rows, inner)
    local_state = (within_state + within_decay * block_start[:, :, None, :]).reshape(
        seq_count, tok_rows, inner
    )
    return (cumulative, local_state, carry_decay, carry_state)


def shards(
    tokens,
    norm_gain,
    lru_proj,
    gelu_proj,
    conv_weight,
    conv_bias,
    gate_weights,
    gate_bias,
    decay_param,
):
    seq_count, tok_rows, width = tokens.shape
    inner = lru_proj.shape[1]
    block_width = gate_weights.shape[1] // 2
    head_count = inner // block_width
    taps = conv_weight.shape[0]
    flat_tokens = tokens.reshape(seq_count * tok_rows, width).astype(jnp.float32)
    mean_square = jnp.mean(flat_tokens * flat_tokens, axis=-1, keepdims=True)
    normed = (flat_tokens * lax.rsqrt(mean_square + 1e-06) * norm_gain).astype(jnp.bfloat16)
    branch = jnp.dot(
        normed,
        lax.all_gather(lru_proj, ("fsdp", "seq"), axis=0, tiled=True),
        preferred_element_type=jnp.float32,
    )
    gelu_in = jnp.dot(
        normed,
        lax.all_gather(gelu_proj, ("fsdp", "seq"), axis=0, tiled=True),
        preferred_element_type=jnp.float32,
    )
    recurrent_in = branch.astype(jnp.bfloat16).reshape(seq_count, tok_rows, inner)
    last_rows = recurrent_in[:, tok_rows - (taps - 1) :, :]
    before = from_behind(last_rows, "seq", 1)
    padded = jnp.concatenate([before, recurrent_in], axis=1)
    conv_sum = jnp.zeros((seq_count, tok_rows, inner), jnp.float32) + conv_bias
    for tap_index in range(taps):
        begin = taps - 1 - tap_index
        conv_sum = conv_sum + conv_weight[tap_index] * padded[
            :, begin : begin + tok_rows, :
        ].astype(jnp.float32)
    conv_out = conv_sum.astype(jnp.bfloat16)
    gate_table = lax.all_gather(gate_weights, "seq", axis=0, tiled=True)
    gate_all = jnp.einsum(
        "nhi,hij->nhj",
        conv_out.reshape(-1, head_count, block_width),
        gate_table.reshape(head_count, block_width, 2 * block_width),
        preferred_element_type=jnp.float32,
    )
    input_gate = jax.nn.sigmoid(
        gate_all[:, :, :block_width].reshape(seq_count, tok_rows, inner) + gate_bias[0]
    )
    recur_gate = jax.nn.sigmoid(
        gate_all[:, :, block_width:].reshape(seq_count, tok_rows, inner) + gate_bias[1]
    )
    log_decay = -8.0 * jax.nn.softplus(decay_param) * recur_gate
    decay = jnp.exp(log_decay)
    driven = jnp.sqrt(-jnp.expm1(2.0 * log_decay)) * input_gate * conv_out.astype(jnp.float32)
    cumulative, local_state, total_decay, end_state = block_scan(decay, driven)
    start_state = jnp.zeros_like(end_state)
    for hop_index in range(lax.axis_size("seq") - 1):
        start_state = from_behind(total_decay * start_state + end_state, "seq", 1)
    state = local_state + cumulative * start_state[:, None, :]
    gelu_part = jax.nn.gelu(gelu_in.reshape(seq_count, tok_rows, inner), approximate=True)
    return (state * gelu_part).astype(jnp.bfloat16)


def solution(mesh):
    placed = (
        P("fsdp", "seq", None),
        P(),
        P(("fsdp", "seq"), None),
        P(("fsdp", "seq"), None),
        P(),
        P(),
        P("seq", None),
        P(),
        P(),
    )
    return jax.shard_map(
        shards, mesh=mesh, in_specs=placed, out_specs=P("fsdp", "seq", None), check_vma=False
    )
```

profile of v0, /device:TPU:1, one launch (start us, length us, event | category | flops | bytes accessed | tf_op | source)
XLA Modules:
  0.0 323.3 jit_solution(12177660864840305348)
XLA Ops:
  8.8 3.1 fusion
  12.0 82.1 %all-gather.4.cloned.1.call-done = bf16[4096,2048]{1,0:T(8,128)(2,1)} async-done(((bf16[32,2048]{1,0:T(8,128)(2,1)}), bf16[4096,2048]{1,0:T(8,128)(2,1)}) %all-gather.4.cloned.1.call-update) | async-done | bytes 16777232 | tf_op jit(solution)/shard_map/all_gather | solution.py:73
  94.1 13.7 %convolution_convert_fusion = bf16[512,2048]{1,0:T(8,128)(2,1)S(1)} fusion(bf16[4096,2048]{1,0:T(8,128)(2,1)} %all-gather.4.cloned.1.call-done, bf16[1,512,4096]{2,1,0:T(8,128)(2,1)} %param.9, f32[4096]{0:T(1024)S(1)} %copy-done.12, f32[512]{0:T(512)S(1)} %add_rsqrt_fusion), kind=kOutput, calls=%fused_computation.27 | convolution fusion | flops 8599371776 | bytes 23087104 | tf_op jit(solution)/shard_map/dot_general | solution.py:71
  107.8 3.0 collective-permute-start
  111.6 2.3 fusion.16
  115.9 5.0 %all-gather.6.cloned.1.call-done = bf16[2048,512]{1,0:T(8,128)(2,1)} async-done(((bf16[256,512]{1,0:T(8,128)(2,1)}), bf16[2048,512]{1,0:T(8,128)(2,1)}) %all-gather.6.cloned.1.call-update) | async-done | bytes 2097168 | tf_op jit(solution)/shard_map/all_gather | solution.py:92
  120.9 3.6 %convolution_bitcast_fusion = f32[512,8,512]{0,2,1:T(8,128)S(1)} fusion(bf16[8,256,512]{2,1,0:T(8,128)(2,1)} %bitcast.2080, bf16[512,8,256]{2,1,0:T(8,128)(2,1)} %bitcast.2079), kind=kOutput, calls=%fused_computation.26 | convolution fusion | flops 1073741824 | bytes 12582912 | tf_op jit(solution)/shard_map/nhi,hij->nhj/dot_general | solution.py:93
  124.5 4.3 %fusion.147 = (f32[512,8,256]{0,2,1:T(8,128)}, f32[512,8,256]{0,2,1:T(8,128)}) fusion(f32[512,8,512]{0,2,1:T(8,128)S(1)} %convolution_bitcast_fusion), kind=kLoop, calls=%fused_computation.555 | loop fusion | bytes 16777216 | tf_op jit(solution)/shard_map/slice | solution.py:103
  128.8 5.5 %copy.83 = f32[512,8,256]{2,1,0:T(8,128)} copy(f32[512,8,256]{0,2,1:T(8,128)} %get-tuple-element.111) | data formatting | bytes 8388608 | tf_op jit(solution)/shard_map/slice | solution.py:103
  134.3 5.4 %copy.275 = f32[1,512,2048]{2,1,0:T(8,128)} copy(f32[1,512,2048]{1,2,0:T(8,128)} %bitcast.2074) | data formatting | bytes 8388608 | tf_op jit(solution)/shard_map/reshape | solution.py:103
  139.7 5.4 %copy.276 = f32[1,512,2048]{2,1,0:T(8,128)} copy(f32[1,512,2048]{1,2,0:T(8,128)} %bitcast.2076) | data formatting | bytes 8388608 | tf_op jit(solution)/shard_map/reshape | solution.py:100
  145.1 4.9 %reshape.9618 = f32[1,8,64,2048]{3,2,1,0:T(8,128)} reshape(f32[512,8,256]{2,1,0:T(8,128)} %copy.83) | data formatting | bytes 8388608 | tf_op jit(solution)/shard_map/reshape | solution.py:103
  150.0 4.0 %multiply_exponential_fusion = f32[1,8,64,2048]{3,2,1,0:T(8,128)S(1)} fusion(f32[1,8,64,2048]{3,2,1,0:T(8,128)} %reshape.9618, f32[2048]{0:T(1024)S(1)} %bitcast.2111, f32[2048]{0:T(1024)S(1)} %fusion.94), kind=kLoop, calls=%fused_computation.24 | loop fusion | flops 5242880 | bytes 8404992 | tf_op jit(solution)/shard_map/exp | solution.py:106
  154.0 3.0 fusion.85
  157.7 4.3 %convert_multiply_fusion.2 = f32[1,512,2048]{2,1,0:T(8,128)S(1)} fusion(bf16[1,512,2048]{2,1,0:T(8,128)(2,1)S(1)} %fusion.16, f32[1,512,2048]{2,1,0:T(8,128)S(1)} %copy-done.4, f32[1,512,2048]{2,1,0:T(8,128)S(1)} %copy-done.3, f32[2048]{0:T(1024)S(1)} %bitcast.2115, f32[2048]{0:T(1024)S(1)} %bitcast.2112, f32[2048]{0:T(1024)S(1)} %fusion.94), kind=kLoop, calls=%fused_computation.25 | loop fusion | flops 14680064 | bytes 14704640 | tf_op jit(solution)/shard_map/mul | solution.py:107
  162.0 6.4 %bitcast_add_fusion.2 = (f32[1,8,2048]{2,0,1:T(1,128)S(1)}, f32[1,8,1,2048]{3,0,2,1:T(1,128)S(1)}, f32[1,8,1,2048]{3,0,2,1:T(1,128)S(1)}, f32[1,8,1,2048]{3,0,2,...) fusion(f32[1,8,64,2048]{3,2,1,0:T(8,128)S(1)} %bitcast.2014, ...), kind=kLoop, calls=%fused_computation.140 | loop fusion | flops 2064384 | bytes 8716288 | tf_op jit(solution)/shard_map/add | solution.py:29
  181.1 2.1 constant_dynamic-update-slice_fusion.37
  184.8 2.1 constant_dynamic-update-slice_fusion.35
  188.5 2.1 constant_dynamic-update-slice_fusion.33
  195.1 2.0 constant_dynamic-update-slice_fusion.29
  198.5 2.0 constant_dynamic-update-slice_fusion.27
  201.8 2.1 constant_dynamic-update-slice_fusion.25
  238.5 3.2 slice_multiply_fusion
  241.7 2.2 fusion.111
  252.5 3.8 %collective-permute-start.3 = (f32[1,2048]{1,0:T(1,128)S(1)}, f32[1,2048]{1,0:T(1,128)S(1)}, u32[]{:S(2)}, u32[]{:S(2)}) collective-permute-start(f32[1,2048]{1,0:T(1,128)S(1)} %multiply_add_fusion.4), channel_id=1, source_target_pairs={{0,1},{1,2},{2,3},{3,4},{4,5},{5,6},{6,7},{8,9},{9,10},{10,11},{11... | collective-permute-start | bytes 24584 | tf_op jit(solution)/shard_map/ppermute | solution.py:10
  257.1 4.2 %collective-permute-start.4 = (f32[1,2048]{1,0:T(1,128)S(1)}, f32[1,2048]{1,0:T(1,128)S(1)}, u32[]{:S(2)}, u32[]{:S(2)}) collective-permute-start(f32[1,2048]{1,0:T(1,128)S(1)} %multiply_add_fusion.3), channel_id=1, source_target_pairs={{0,1},{1,2},{2,3},{3,4},{4,5},{5,6},{6,7},{8,9},{9,10},{10,11},{11... | collective-permute-start | bytes 24584 | tf_op jit(solution)/shard_map/ppermute | solution.py:10
  262.1 4.2 %collective-permute-start.5 = (f32[1,2048]{1,0:T(1,128)S(1)}, f32[1,2048]{1,0:T(1,128)S(1)}, u32[]{:S(2)}, u32[]{:S(2)}) collective-permute-start(f32[1,2048]{1,0:T(1,128)S(1)} %multiply_add_fusion.2), channel_id=1, source_target_pairs={{0,1},{1,2},{2,3},{3,4},{4,5},{5,6},{6,7},{8,9},{9,10},{10,11},{11... | collective-permute-start | bytes 24584 | tf_op jit(solution)/shard_map/ppermute | solution.py:10
  267.1 4.2 %collective-permute-start.6 = (f32[1,2048]{1,0:T(1,128)S(1)}, f32[1,2048]{1,0:T(1,128)S(1)}, u32[]{:S(2)}, u32[]{:S(2)}) collective-permute-start(f32[1,2048]{1,0:T(1,128)S(1)} %multiply_add_fusion.1), channel_id=1, source_target_pairs={{0,1},{1,2},{2,3},{3,4},{4,5},{5,6},{6,7},{8,9},{9,10},{10,11},{11... | collective-permute-start | bytes 24584 | tf_op jit(solution)/shard_map/ppermute | solution.py:10
  272.1 4.2 %collective-permute-start.7 = (f32[1,2048]{1,0:T(1,128)S(1)}, f32[1,2048]{1,0:T(1,128)S(1)}, u32[]{:S(2)}, u32[]{:S(2)}) collective-permute-start(f32[1,2048]{1,0:T(1,128)S(1)} %multiply_add_fusion), channel_id=1, source_target_pairs={{0,1},{1,2},{2,3},{3,4},{4,5},{5,6},{6,7},{8,9},{9,10},{10,11},{11... | collective-permute-start | bytes 24584 | tf_op jit(solution)/shard_map/ppermute | solution.py:10
  278.2 3.9 %copy.277 = f32[1,8,64,2048]{3,2,0,1:T(8,128)} copy(f32[1,8,64,2048]{3,0,2,1:T(1,128)S(1)} %constant_dynamic-update-slice_fusion) | data formatting | bytes 8388608
  282.2 15.1 %stack.14 = f32[1,8,64,2048]{3,2,1,0:T(8,128)} concatenate(f32[1,8,1,2048]{3,2,1,0:T(1,128)} %slice.766, f32[1,8,1,2048]{3,2,1,0:T(1,128)S(1)} %get-tuple-element.139, f32[1,8,1,2048]{3,2,1,0:T(1,128)S(1)} %bitcast.2084, f32[1,8,1,2048]{3,2,1,0:T(1,128)S(1)} %get-tuple-element.137, f32[1,8,1,2048]{3,2,1,0:T(1,128)S(1)} %bitcast.2083, f32[1,8,1,2048]{3,2,1,0:T(1,128)S(1)} %get-tuple-element.135, ...), dimensions={2} | concatenate | bytes 8388608 | tf_op jit(solution)/shard_map/stack | solution.py:32
  297.3 19.3 %fusion.11 = bf16[512,2048]{1,0:T(8,128)(2,1)} fusion(f32[1,8,64,2048]{3,2,0,1:T(8,128)} %copy.277, f32[1,8,64,2048]{3,2,1,0:T(8,128)} %stack.14, f32[2048]{0:T(1024)S(1)} %bitcast.2120, f32[8,2048]{1,0:T(8,128)} %bitcast.2113, f32[8,2048]{1,0:T(8,128)} %bitcast.2114, bf16[4096,2048]{1,0:T(8,128)(2,1)} %all-gather.8.cloned.1.call-done, ...), kind=kOutput, calls=%fused_computation.14 | convolution fusion | flops 8614051840 | bytes 31614976 | tf_op jit(solution)/shard_map/dot_general | solution.py:76
  (135 shorter events, 76.9 us)
Async XLA Ops:
  6.5 5.3 %copy-start.8 = (f32[4,2048]{1,0:T(4,128)S(1)}, f32[4,2048]{1,0:T(4,128)}, u32[]{:S(2)}) copy-start(f32[4,2048]{1,0:T(4,128)} %param.13) | copy-start | bytes 98308
  6.5 5.4 %copy-start.9 = (f32[2,2048]{1,0:T(2,128)S(1)}, f32[2,2048]{1,0:T(2,128)}, u32[]{:S(2)}) copy-start(f32[2,2048]{1,0:T(2,128)} %param.16) | copy-start | bytes 49156
  6.5 5.4 %copy-start.11 = (f32[2048]{0:T(1024)S(1)}, f32[2048]{0:T(1024)}, u32[]{:S(2)}) copy-start(f32[2048]{0:T(1024)} %param.17) | copy-start | bytes 24580
  6.5 87.6 %copy-start.12 = (f32[4096]{0:T(1024)S(1)}, f32[4096]{0:T(1024)}, u32[]{:S(2)}) copy-start(f32[4096]{0:T(1024)} %param.10) | copy-start | bytes 49156
  6.5 87.6 %all-gather.4.cloned.1.call-start = ((), (), s32[]{:S(2)}) async-start(), calls=%async_computation | async-start | bytes 16908288 | tf_op jit(solution)/shard_map/all_gather | solution.py:73
  7.3 113.6 %all-gather.6.cloned.1.call-start = ((), (), s32[]{:S(2)}) async-start(), calls=%async_computation.1 | async-start | bytes 2359296 | tf_op jit(solution)/shard_map/all_gather | solution.py:92
  8.0 289.2 %all-gather.8.cloned.1.call-start = ((), (), s32[]{:S(2)}) async-start(), calls=%async_computation.2 | async-start | bytes 16908288 | tf_op jit(solution)/shard_map/all_gather | solution.py:78
  12.0 99.6 %copy-start.10 = (f32[2048]{0:T(1024)S(1)}, f32[2048]{0:T(1024)}, u32[]{:S(2)}) copy-start(f32[2048]{0:T(1024)} %param.14) | copy-start | bytes 24580
  107.8 3.7 %collective-permute-start = (bf16[1,3,2048]{2,1,0:T(4,128)(2,1)S(1)}, bf16[1,3,2048]{2,1,0:T(4,128)(2,1)S(1)}, u32[]{:S(2)}, u32[]{:S(2)}) collective-permute-start(bf16[1,3,2048]{2,1,0:T(4,128)(2,1)S(1)} %slice.632), channel_id=1, source_target_pairs={{0,1},{1,2},{2,3},{3,4},{4,5},{5,6},{6,7},{8,9},{9,10},{10,11},{11... | collective-permute-start | bytes 36872 | tf_op jit(solution)/shard_map/ppermute | solution.py:10
  150.0 7.0 %copy-start.4 = (f32[1,512,2048]{2,1,0:T(8,128)S(1)}, f32[1,512,2048]{2,1,0:T(8,128)}, u32[]{:S(2)}) copy-start(f32[1,512,2048]{2,1,0:T(8,128)} %copy.276) | copy-start | bytes 12582916
  154.0 19.1 %copy-start = (f32[1,8,64,2048]{3,2,1,0:T(8,128)}, f32[1,8,64,2048]{3,2,1,0:T(8,128)S(1)}, u32[]{:S(2)}) copy-start(f32[1,8,64,2048]{3,2,1,0:T(8,128)S(1)} %multiply_exponential_fusion) | copy-start | bytes 12582916
  154.0 3.7 %copy-start.3 = (f32[1,512,2048]{2,1,0:T(8,128)S(1)}, f32[1,512,2048]{2,1,0:T(8,128)}, u32[]{:S(2)}) copy-start(f32[1,512,2048]{2,1,0:T(8,128)} %copy.275) | copy-start | bytes 12582916
  162.0 11.1 %copy-start.2 = (f32[1,512,2048]{2,1,0:T(8,128)}, f32[1,512,2048]{2,1,0:T(8,128)S(1)}, u32[]{:S(2)}) copy-start(f32[1,512,2048]{2,1,0:T(8,128)S(1)} %convert_multiply_fusion.2) | copy-start | bytes 12582916
  168.6 80.7 %collective-permute-start.1 = (f32[1,2048]{1,0:T(1,128)S(1)}, f32[1,2048]{1,0:T(1,128)S(1)}, u32[]{:S(2)}, u32[]{:S(2)}) collective-permute-start(f32[1,2048]{1,0:T(1,128)S(1)} %get-tuple-element.15), channel_id=1, source_target_pairs={{0,1},{1,2},{2,3},{3,4},{4,5},{5,6},{6,7},{8,9},{9,10},{10,11},{11... | collective-permute-start | bytes 24584 | tf_op jit(solution)/shard_map/ppermute | solution.py:10
  171.9 28.6 %copy-start.6 = (f32[1,8,2048]{2,0,1:T(1,128)}, f32[1,8,2048]{2,0,1:T(1,128)S(1)}, u32[]{:S(2)}) copy-start(f32[1,8,2048]{2,0,1:T(1,128)S(1)} %constant_dynamic-update-slice_fusion.66) | copy-start | bytes 196612
  201.8 36.7 %copy-start.1 = (f32[1,8,64,2048]{3,2,1,0:T(8,128)S(1)}, f32[1,8,64,2048]{3,2,1,0:T(8,128)}, u32[]{:S(2)}) copy-start(f32[1,8,64,2048]{3,2,1,0:T(8,128)} %copy-done) | copy-start | bytes 12582916
  241.7 7.7 %copy-start.5 = (f32[1,8,2048]{2,0,1:T(1,128)S(1)}, f32[1,8,2048]{2,0,1:T(1,128)}, u32[]{:S(2)}) copy-start(f32[1,8,2048]{2,0,1:T(1,128)} %constant_dynamic-update-slice_fusion.79) | copy-start | bytes 196612
  241.7 7.7 %copy-start.7 = (f32[1,8,2048]{2,0,1:T(1,128)S(1)}, f32[1,8,2048]{2,0,1:T(1,128)}, u32[]{:S(2)}) copy-start(f32[1,8,2048]{2,0,1:T(1,128)} %copy-done.6) | copy-start | bytes 196612
  249.4 3.1 collective-permute-start.2
  252.5 4.6 %collective-permute-start.3 = (f32[1,2048]{1,0:T(1,128)S(1)}, f32[1,2048]{1,0:T(1,128)S(1)}, u32[]{:S(2)}, u32[]{:S(2)}) collective-permute-start(f32[1,2048]{1,0:T(1,128)S(1)} %multiply_add_fusion.4), channel_id=1, source_target_pairs={{0,1},{1,2},{2,3},{3,4},{4,5},{5,6},{6,7},{8,9},{9,10},{10,11},{11... | collective-permute-start | bytes 24584 | tf_op jit(solution)/shard_map/ppermute | solution.py:10
  257.1 5.0 %collective-permute-start.4 = (f32[1,2048]{1,0:T(1,128)S(1)}, f32[1,2048]{1,0:T(1,128)S(1)}, u32[]{:S(2)}, u32[]{:S(2)}) collective-permute-start(f32[1,2048]{1,0:T(1,128)S(1)} %multiply_add_fusion.3), channel_id=1, source_target_pairs={{0,1},{1,2},{2,3},{3,4},{4,5},{5,6},{6,7},{8,9},{9,10},{10,11},{11... | collective-permute-start | bytes 24584 | tf_op jit(solution)/shard_map/ppermute | solution.py:10
  262.1 5.0 %collective-permute-start.5 = (f32[1,2048]{1,0:T(1,128)S(1)}, f32[1,2048]{1,0:T(1,128)S(1)}, u32[]{:S(2)}, u32[]{:S(2)}) collective-permute-start(f32[1,2048]{1,0:T(1,128)S(1)} %multiply_add_fusion.2), channel_id=1, source_target_pairs={{0,1},{1,2},{2,3},{3,4},{4,5},{5,6},{6,7},{8,9},{9,10},{10,11},{11... | collective-permute-start | bytes 24584 | tf_op jit(solution)/shard_map/ppermute | solution.py:10
  267.1 5.0 %collective-permute-start.6 = (f32[1,2048]{1,0:T(1,128)S(1)}, f32[1,2048]{1,0:T(1,128)S(1)}, u32[]{:S(2)}, u32[]{:S(2)}) collective-permute-start(f32[1,2048]{1,0:T(1,128)S(1)} %multiply_add_fusion.1), channel_id=1, source_target_pairs={{0,1},{1,2},{2,3},{3,4},{4,5},{5,6},{6,7},{8,9},{9,10},{10,11},{11... | collective-permute-start | bytes 24584 | tf_op jit(solution)/shard_map/ppermute | solution.py:10
  272.1 25.2 %collective-permute-start.7 = (f32[1,2048]{1,0:T(1,128)S(1)}, f32[1,2048]{1,0:T(1,128)S(1)}, u32[]{:S(2)}, u32[]{:S(2)}) collective-permute-start(f32[1,2048]{1,0:T(1,128)S(1)} %multiply_add_fusion), channel_id=1, source_target_pairs={{0,1},{1,2},{2,3},{3,4},{4,5},{5,6},{6,7},{8,9},{9,10},{10,11},{11... | collective-permute-start | bytes 24584 | tf_op jit(solution)/shard_map/ppermute | solution.py:10
  282.2 15.1 %copy-start.13 = (f32[4096]{0:T(1024)S(1)}, f32[4096]{0:T(1024)}, u32[]{:S(2)}) copy-start(f32[4096]{0:T(1024)} %param.10) | copy-start | bytes 49156
Sparse Core Ops, SparseCore 0:
  10.5 83.5 all-gather.3
  95.8 24.9 all-gather.5
  124.0 80.2 all-gather.7
where the time goes:
time: 329 us; the launch traced here: 323 us
  other arithmetic  102 us (31%)
  waiting for transfers between devices  93.4 us (28%)
  local copies, waits for them, and re-layouts  50 us (15%)
  matrix products  36.6 us (11%)
  starting transfers between devices  27.6 us (8%)
  between operations  13.8 us (4%)
    all_gather x1, waiting for transfers between devices, shards(): lax.all_gather(lru_proj, ('fsdp', 'seq'), axis=0, tiled=True)  82.1 us
    unnamed x66, other arithmetic  69.3 us
    ppermute x8, starting transfers between devices, from_behind(): return lax.ppermute(x, axis, pairs)  27.5 us
    dot_general x1, matrix products, shards(): jnp.dot(normed, lax.all_gather(gelu_proj, ('fsdp', 'seq'), axis=0, tiled=...  19.3 us
    another operation x1, local copies, waits for them, and re-layouts, block_scan(): within_decay = jnp.stack(decay_list, axis=2)  15.1 us
    dot_general x1, matrix products, shards(): jnp.dot(normed, lax.all_gather(lru_proj, ('fsdp', 'seq'), axis=0, tiled=T...  13.7 us
    mul x6, other arithmetic, block_scan(): running_decay = running_decay * decay_now  11.2 us
    reshape x2, local copies, waits for them, and re-layouts, shards(): gate_all[:, :, block_width:].reshape(seq_count, tok_rows, inner)  10.3 us
  transfers between devices with their start and end apart: 11, of which 8 were waited for; matrix products, arithmetic and copies ran while one was open for 52% of the time, Pallas kernels for 0%

commit v1 on v0

v1 whole, which is shorter than its diff:
```python
import jax
import jax.numpy as jnp
from jax import lax
from jax.experimental import pallas as pl
from jax.experimental.pallas import tpu as pltpu
from jax.sharding import PartitionSpec as P

MESH = pl.DeviceIdType.MESH
HALO = 16
ROWS = 1024
WIDTH = 4096
HEADS = 4
BW = 256
CHUNKS = 8
X, Y, Z = 0, 1, 2
ORDERS = ((X, Y, Z), (Y, Z, X), (Z, X, Y))
PIECES = (
    (slice(0, 16), slice(0, 256)),
    (slice(16, 64), slice(0, 128)),
    (slice(16, 64), slice(128, 256)),
)
L_ROWS = 208
T_ROWS = 128
G_ROWS = 256


def piece(w, chunks, colour, phase, coords, half=None):
    order = ORDERS[colour]
    at = [chunks, None, None, None]
    for place, dim in enumerate(order):
        if place < phase:
            at[1 + dim] = pl.ds(0, 4)
            if place == 0 and half is not None:
                at[1 + dim] = pl.ds(2 * half, 2)
        else:
            at[1 + dim] = coords[dim]
    rows, cols = PIECES[colour]
    at.append(pl.ds(rows.start, rows.stop - rows.start))
    at.append(pl.ds(cols.start, cols.stop - cols.start))
    return w.at[tuple(at)]


def moved(coords, dim, by):
    new = list(coords)
    new[dim] = lax.rem(coords[dim] + (by + 4), 4)
    return new


class Ring:
    def __init__(self, w, chunks, colour, phase, coords, core, send, recv):
        self.w, self.chunks, self.colour, self.phase = w, chunks, colour, phase
        self.coords, self.core, self.send, self.recv = coords, core, send, recv
        self.dim = ORDERS[colour][phase]

    def device(self, by):
        x, y, z = moved(self.coords, self.dim, by)
        return (x * 4 + y, z * 2 + self.core)

    def block(self, by, half=None):
        chunks = self.chunks
        if self.phase == 0 and half is not None:
            chunks = pl.ds(4 * half, 4)
            half = None
        return piece(self.w, chunks, self.colour, self.phase, moved(self.coords, self.dim, by), half)

    def copy(self, hop, side, outgoing):
        way = 1 - 2 * side
        half = None if hop == 0 else side
        if outgoing:
            ref = self.block(-way * hop, half)
        else:
            ref = self.block(-way * (hop + 1), half)
        return pltpu.make_async_remote_copy(
            src_ref=ref,
            dst_ref=ref,
            send_sem=self.send.at[hop, side],
            recv_sem=self.recv.at[hop, side],
            device_id=self.device(way),
            device_id_type=MESH,
        )

    def start(self, hop):
        for side in range(2):
            self.copy(hop, side, True).start()

    def wait(self, hop):
        for side in range(2):
            self.copy(hop, side, False).wait_recv()

    def drain(self, hop):
        for side in range(2):
            self.copy(hop, side, True).wait_send()


def softplus_of(value):
    return jnp.maximum(value, 0.0) + jnp.log1p(jnp.exp(-jnp.abs(value)))


def one_minus_square(decay, twice):
    series = 1.0 + twice * (1.0 / 7.0)
    for divisor in (6.0, 5.0, 4.0, 3.0, 2.0):
        series = 1.0 + twice * (1.0 / divisor) * series
    return jnp.where(twice > -0.3, -twice * series, 1.0 - decay * decay)


def tile_scan(decay, driven):
    rows, cols = decay.shape
    place = lax.broadcasted_iota(jnp.int32, (rows, cols), 0)
    for step in (1, 2, 4):
        inside = (place % 8) >= step
        a_prev = jnp.where(inside, pltpu.roll(decay, step, 0), 1.0)
        b_prev = jnp.where(inside, pltpu.roll(driven, step, 0), 0.0)
        driven = decay * b_prev + driven
        decay = decay * a_prev
    group = decay.reshape(rows // 8, 8, cols)
    state = driven.reshape(rows // 8, 8, cols)
    last_a = jnp.broadcast_to(group[:, 7:8, :], group.shape)
    last_b = jnp.broadcast_to(state[:, 7:8, :], state.shape)
    run_a, run_b = last_a, last_b
    step = 1
    while step < rows // 8:
        ones = jnp.ones((step, 8, cols), jnp.float32)
        zeros = jnp.zeros((step, 8, cols), jnp.float32)
        a_prev = jnp.concatenate([ones, run_a[:-step]], axis=0)
        b_prev = jnp.concatenate([zeros, run_b[:-step]], axis=0)
        run_b = run_a * b_prev + run_b
        run_a = run_a * a_prev
        step *= 2
    ones = jnp.ones((1, 8, cols), jnp.float32)
    zeros = jnp.zeros((1, 8, cols), jnp.float32)
    before_a = jnp.concatenate([ones, run_a[:-1]], axis=0)
    before_b = jnp.concatenate([zeros, run_b[:-1]], axis=0)
    state = (state + group * before_b).reshape(rows, cols)
    group = (group * before_a).reshape(rows, cols)
    return group, state, run_a[-1], run_b[-1]


def body(
    tokens, gain, lru, gelu, conv_w, conv_b, gates, gate_b, decay_p, out,
    xn, w, gate_v, rec, local, cumul, outs, ends,
    own_sem, p1_send, p1_recv, p2_send, p2_recv, p3_send, p3_recv,
    tok_sem, halo_sem, gate_send, gate_recv, end_send, end_recv, out_sem, out_recv,
):
    fsdp = lax.axis_index("fsdp")
    seq = lax.axis_index("seq")
    x, y = fsdp // 4, fsdp % 4
    z, core = seq // 2, seq % 2
    other = 1 - core
    coords = [x, y, z]
    partner = (fsdp, z * 2 + other)

    barrier = pltpu.get_barrier_semaphore()
    for dim in (X, Y):
        for by in (1, -1):
            nx, ny, nz = moved(coords, dim, by)
            pl.semaphore_signal(
                barrier, inc=1, device_id=(nx * 4 + ny, nz * 2 + core), device_id_type=MESH
            )
    for by in range(1, 8):
        pl.semaphore_signal(
            barrier, inc=1, device_id=(fsdp, lax.rem(seq + by, 8)), device_id_type=MESH
        )

    def own_copies(mine):
        found = []
        for mat, source in enumerate((lru, gelu)):
            for head in range(HEADS):
                side = core if mine else other
                first = pl.multiple_of(side * (HEADS * BW) + head * BW, BW)
                found.append(
                    (
                        source.at[:, pl.ds(first, BW)],
                        w.at[2 * head + mat, x, y, z, pl.ds(pl.multiple_of(core * 32, 32), 32), :],
                        2 * head + mat,
                    )
                )
        return found

    local_copies = [
        pltpu.make_async_copy(src, dst, own_sem.at[0, n]) for src, dst, n in own_copies(True)
    ]
    for copy in local_copies:
        copy.start()
    my_rows = pl.ds(pl.multiple_of(HALO + core * 512, 16), 512)
    my_tokens = pltpu.make_async_copy(tokens.at[0], xn.at[my_rows, :], tok_sem.at[0])
    my_tokens.start()

    pl.semaphore_wait(barrier, 11)

    far_copies = [
        pltpu.make_async_remote_copy(
            src_ref=src,
            dst_ref=dst,
            send_sem=own_sem.at[1, n],
            recv_sem=own_sem.at[2, n],
            device_id=partner,
            device_id_type=MESH,
        )
        for src, dst, n in own_copies(False)
    ]
    for copy in far_copies:
        copy.start()
    for n, copy in enumerate(local_copies):
        copy.wait()
    other_rows = pl.ds(pl.multiple_of(other * 32, 32), 32)
    for n in range(CHUNKS):
        landed = w.at[n, x, y, z, other_rows, :]
        pltpu.make_async_copy(landed, landed, own_sem.at[2, n]).wait()

    def ring(phase, n, colour):
        send, recv = ((p1_send, p1_recv), (p2_send, p2_recv), (p3_send, p3_recv))[phase]
        if phase == 0:
            return Ring(w, pl.ds(0, CHUNKS), colour, 0, coords, core, send.at[colour], recv.at[colour])
        return Ring(w, n, colour, phase, coords, core, send.at[colour], recv.at[n, colour])

    def start(phase, n, hop):
        for colour in range(3):
            ring(phase, n, colour).start(hop)

    def wait(phase, n, hop):
        for colour in range(3):
            ring(phase, n, colour).wait(hop)

    start(0, None, 0)

    give_tokens = pltpu.make_async_remote_copy(
        src_ref=tokens.at[0],
        dst_ref=xn.at[my_rows, :],
        send_sem=tok_sem.at[1],
        recv_sem=tok_sem.at[2],
        device_id=partner,
        device_id_type=MESH,
    )
    give_tokens.start()

    def halo_copy(to_core):
        return pltpu.make_async_remote_copy(
            src_ref=tokens.at[0, pl.ds(512 - HALO, HALO), :],
            dst_ref=xn.at[pl.ds(0, HALO), :],
            send_sem=halo_sem.at[to_core],
            recv_sem=halo_sem.at[2],
            device_id=(fsdp, lax.rem(z + 1, 4) * 2 + to_core),
            device_id_type=MESH,
        )

    @pl.when(core == 1)
    def _():
        halo_copy(0).start()
        halo_copy(1).start()

    wait(0, None, 0)
    start(0, None, 1)

    kind = z // 2
    slot = (z % 2) * 2 + core

    def gate_copy(by):
        return pltpu.make_async_remote_copy(
            src_ref=gates,
            dst_ref=gate_v.at[slot],
            send_sem=gate_send.at[by],
            recv_sem=gate_recv.at[slot],
            device_id=(fsdp, lax.rem(z + by, 4) * 2 + kind),
            device_id_type=MESH,
        )

    def gate_local():
        return pltpu.make_async_copy(gates, gate_v.at[slot], gate_recv.at[slot])

    @pl.when(core == kind)
    def _():
        gate_local().start()

    @pl.when(core != kind)
    def _():
        gate_copy(0).start()

    wait(0, None, 1)
    start(1, 0, 0)
    start(1, 1, 0)
    start(1, 2, 0)
    for by in range(1, 4):
        gate_copy(by).start()

    my_tokens.wait()
    give_tokens.wait_recv()
    halo_copy(0).wait_recv()

    wait(1, 0, 0)
    start(1, 0, 1)
    wait(1, 1, 0)
    start(1, 1, 1)

    def norm_tile(i, _):
        rows = pl.ds(pl.multiple_of(i * 16, 16), 16)
        value = xn[rows, :].astype(jnp.float32)
        mean = jnp.mean(value * value, axis=-1, keepdims=True)
        normed = value * lax.rsqrt(mean + 1e-06) * gain[...]
        keep = jnp.where(jnp.logical_and(i == 0, z == 0), 0.0, 1.0)
        xn[rows, :] = (normed * keep).astype(jnp.bfloat16)
        return 0

    def norm(first, last):
        lax.fori_loop(first, last, norm_tile, 0)

    norm(0, 20)
    wait(1, 0, 1)
    start(2, 0, 0)
    wait(1, 2, 0)
    start(1, 2, 1)
    start(1, 3, 0)
    norm(20, 65)

    def columns(head):
        return pl.ds(pl.multiple_of(core * (HEADS * BW) + head * BW, BW), BW)

    def lru_chunk(head):
        n = 2 * head

        def rows_of(i, _):
            rows = pl.ds(pl.multiple_of(i * L_ROWS, 16), L_ROWS)
            value = jnp.dot(
                xn[rows, :], w[n].reshape(WIDTH, BW), preferred_element_type=jnp.float32
            )
            rec[rows, :] = value.astype(jnp.bfloat16).astype(jnp.float32)
            return 0

        lax.fori_loop(0, (HALO + ROWS) // L_ROWS, rows_of, 0)
        cols = columns(head)
        taps = conv_w[:, cols]
        bias = conv_b[:, cols]
        g_bias = gate_b[:, cols]
        rate = -8.0 * softplus_of(decay_p[:, cols])
        gate_block = gates_of(head)

        def tile(i, carry):
            carry_a, carry_b = carry
            first = pl.multiple_of(i * T_ROWS + (HALO - 8), 8)
            value = rec[pl.ds(first, T_ROWS + 8), :]
            total = jnp.zeros((T_ROWS, BW), jnp.float32) + bias
            for tap in range(4):
                total = total + taps[tap : tap + 1, :] * value[8 - tap : 8 - tap + T_ROWS, :]
            conv = total.astype(jnp.bfloat16)
            gate = jnp.dot(conv, gate_block, preferred_element_type=jnp.float32)
            input_gate = jax.nn.sigmoid(gate[:, :BW] + g_bias[0:1, :])
            recur_gate = jax.nn.sigmoid(gate[:, BW:] + g_bias[1:2, :])
            log_decay = rate * recur_gate
            decay = jnp.exp(log_decay)
            driven = (
                jnp.sqrt(one_minus_square(decay, 2.0 * log_decay))
                * input_gate
                * conv.astype(jnp.float32)
            )
            within_a, within_b, tile_a, tile_b = tile_scan(decay, driven)
            rows = pl.ds(pl.multiple_of(i * T_ROWS, T_ROWS), T_ROWS)
            local[head % 2, rows, :] = within_b + within_a * carry_b[0:1, :]
            cumul[head % 2, rows, :] = within_a * carry_a[0:1, :]
            return tile_a * carry_a, tile_b + tile_a * carry_b

        begin = (jnp.ones((8, BW), jnp.float32), jnp.zeros((8, BW), jnp.float32))
        end_a, end_b = lax.fori_loop(0, ROWS // T_ROWS, tile, begin)
        ends[head, z, 0, :, :] = end_a
        ends[head, z, 1, :, :] = end_b

    def gates_of(head):
        return gate_v[head]

    def end_copy(head, by):
        return pltpu.make_async_remote_copy(
            src_ref=ends.at[head, z],
            dst_ref=ends.at[head, z],
            send_sem=end_send.at[head, by - 1],
            recv_sem=end_recv.at[head, by - 1],
            device_id=(fsdp, lax.rem(z + by, 4) * 2 + core),
            device_id_type=MESH,
        )

    def end_landed(head, by):
        source = lax.rem(z + 4 - by, 4)
        landed = ends.at[head, source]
        pltpu.make_async_copy(landed, landed, end_recv.at[head, by - 1]).wait()

    def out_copy(head, i, far):
        side = other if far else core
        src = outs.at[head, pl.ds(pl.multiple_of(side * 512 + i * G_ROWS, G_ROWS), G_ROWS), :]
        dst = out.at[0, pl.ds(i * G_ROWS, G_ROWS), columns(head)]
        if far:
            return pltpu.make_async_remote_copy(
                src_ref=src,
                dst_ref=dst,
                send_sem=out_sem.at[1, head, i],
                recv_sem=out_recv.at[head, i],
                device_id=partner,
                device_id_type=MESH,
            )
        return pltpu.make_async_copy(src, dst, out_sem.at[0, head, i])

    def gelu_chunk(head):
        n = 2 * head + 1
        for by in range(1, 4):
            end_landed(head, by)
        begin = jnp.zeros((8, BW), jnp.float32)
        for source in range(3):
            after = ends[head, source, 0] * begin + ends[head, source, 1]
            begin = jnp.where(source < z, after, begin)
        weight = w[n].reshape(WIDTH, BW)
        for far in (True, False):
            side = other if far else core
            for i in range(2):
                first = pl.multiple_of(side * 512 + i * G_ROWS, G_ROWS)
                rows = pl.ds(first, G_ROWS)
                gelu_in = jnp.dot(
                    xn[pl.ds(pl.multiple_of(first + HALO, 16), G_ROWS), :],
                    weight,
                    preferred_element_type=jnp.float32,
                )
                state = local[head % 2, rows, :] + cumul[head % 2, rows, :] * begin[0:1, :]
                inner = gelu_in * (
                    0.7978845608028654 + (0.7978845608028654 * 0.044715) * (gelu_in * gelu_in)
                )
                part = 0.5 * gelu_in * (1.0 + jnp.tanh(inner))
                outs[head, rows, :] = (state * part).astype(jnp.bfloat16)
                out_copy(head, i, far).start()

    for j in range(4):
        landed = gate_v.at[j]
        if j == 0:
            pass

    def compute(n):
        head = n // 2
        if n == 0:
            for j in range(HEADS):
                pltpu.make_async_copy(gate_v.at[j], gate_v.at[j], gate_recv.at[j]).wait()
        if n % 2 == 0:
            lru_chunk(head)
            for by in range(1, 4):
                end_copy(head, by).start()
        else:
            gelu_chunk(head)

    for k in range(CHUNKS + 1):
        if k + 1 < CHUNKS:
            wait(1, k + 1, 1)
            start(2, k + 1, 0)
        if k < CHUNKS:
            wait(2, k, 0)
            start(2, k, 1)
        if k + 4 < CHUNKS:
            start(1, k + 4, 0)
        if k + 3 < CHUNKS:
            wait(1, k + 3, 0)
            start(1, k + 3, 1)
        if k >= 1:
            wait(2, k - 1, 1)
            compute(k - 1)

    for head in range(HEADS):
        for i in range(2):
            out_copy(head, i, False).wait()
            out_copy(head, i, True).wait_send()
            landed = out.at[0, pl.ds(i * G_ROWS, G_ROWS), pl.ds(pl.multiple_of(other * (HEADS * BW) + head * BW, BW), BW)]
            pltpu.make_async_copy(landed, landed, out_recv.at[head, i]).wait()
        for by in range(1, 4):
            end_copy(head, by).wait_send()
    for copy in far_copies:
        copy.wait_send()
    give_tokens.wait_send()

    @pl.when(core == 1)
    def _():
        halo_copy(0).wait_send()
        halo_copy(1).wait_send()

    @pl.when(core != kind)
    def _():
        gate_copy(0).wait_send()

    for by in range(1, 4):
        gate_copy(by).wait_send()
    for phase in range(3):
        send = (p1_send, p2_send, p3_send)[phase]
        for colour in range(3):
            every = Ring(w, pl.ds(0, CHUNKS), colour, phase, coords, core, send.at[colour], send.at[colour])
            for hop in range(2):
                every.drain(hop)


def shards(tokens, norm_gain, lru, gelu, conv_weight, conv_bias, gates, gate_bias, decay_param):
    dma = pltpu.SemaphoreType.DMA
    hbm = pl.BlockSpec(memory_space=pl.ANY)
    vmem = pl.BlockSpec(memory_space=pltpu.VMEM)
    return pl.pallas_call(
        body,
        name="branch",
        out_shape=jax.ShapeDtypeStruct((1, 512, 2048), jnp.bfloat16),
        in_specs=[hbm, vmem, hbm, hbm, vmem, vmem, hbm, vmem, vmem],
        out_specs=hbm,
        scratch_shapes=[
            pltpu.VMEM((HALO + ROWS, WIDTH), jnp.bfloat16),
            pltpu.VMEM((CHUNKS, 4, 4, 4, 64, BW), jnp.bfloat16),
            pltpu.VMEM((HEADS, BW, 2 * BW), jnp.bfloat16),
            pltpu.VMEM((HALO + ROWS, BW), jnp.float32),
            pltpu.VMEM((2, ROWS, BW), jnp.float32),
            pltpu.VMEM((2, ROWS, BW), jnp.float32),
            pltpu.VMEM((HEADS, ROWS, BW), jnp.bfloat16),
            pltpu.VMEM((HEADS, 4, 2, 8, BW), jnp.float32),
            dma((3, CHUNKS)),
            dma((3, 2, 2)),
            dma((3, 2, 2)),
            dma((3, 2, 2)),
            dma((CHUNKS, 3, 2, 2)),
            dma((3, 2, 2)),
            dma((CHUNKS, 3, 2, 2)),
            dma((3,)),
            dma((3,)),
            dma((4,)),
            dma((4,)),
            dma((HEADS, 3)),
            dma((HEADS, 3)),
            dma((2, HEADS, 2)),
            dma((HEADS, 2)),
        ],
        compiler_params=pltpu.CompilerParams(
            collective_id=0, has_side_effects=True, vmem_limit_bytes=60 * 1024 * 1024
        ),
    )(
        tokens,
        norm_gain.reshape(1, -1),
        lru,
        gelu,
        conv_weight,
        conv_bias.reshape(1, -1),
        gates,
        gate_bias,
        decay_param.reshape(1, -1),
    )


def solution(mesh):
    placed = (
        P("fsdp", "seq", None),
        P(),
        P(("fsdp", "seq"), None),
        P(("fsdp", "seq"), None),
        P(),
        P(),
        P("seq", None),
        P(),
        P(),
    )
    return jax.shard_map(
        shards, mesh=mesh, in_specs=placed, out_specs=P("fsdp", "seq", None), check_vma=False
    )
```

time: 329 us -> 125 us (0.38); the launches traced: 323 us -> 125 us
  Pallas kernels: 0 us -> 122 us
  other arithmetic: 102 us -> 0 us
  waiting for transfers between devices: 93.4 us -> 0 us
  local copies, waits for them, and re-layouts: 50 us -> 3.16 us
  matrix products: 36.6 us -> 0 us
  starting transfers between devices: 27.6 us -> 0 us
  between operations: 13.8 us -> 0.01 us
    pallas_call x0 -> x1, Pallas kernels: none -> 122 us  [shards(): pl.pallas_call(body, name='branch', out_shape=jax.ShapeDtypeStruct((1, 51...]
    all_gather x3 -> x0, waiting for transfers between devices: 87.1 us -> none  [the longest x1 82.1 us: shards(): lax.all_gather(lru_proj, ('fsdp', 'seq'), axis=0, tiled=True)]
    unnamed x66 -> x0, other arithmetic: 69.3 us -> none
    dot_general x3 -> x0, matrix products: 36.6 us -> none  [the longest x1 19.3 us: shards(): jnp.dot(normed, lax.all_gather(gelu_proj, ('fsdp', 'seq'), axis=0, tiled=...]
    ppermute x8 -> x0, starting transfers between devices: 27.5 us -> none  [from_behind(): return lax.ppermute(x, axis, pairs)]
    reshape x3 -> x0, local copies, waits for them, and re-layouts: 15.7 us -> none  [the longest x2 10.3 us: shards(): gate_all[:, :, block_width:].reshape(seq_count, tok_rows, inner)]
    mul x8 -> x0, other arithmetic: 15.5 us -> none  [the longest x6 11.2 us: block_scan(): running_decay = running_decay * decay_now]
    another operation x1 -> x0, local copies, waits for them, and re-layouts: 15.1 us -> none  [block_scan(): within_decay = jnp.stack(decay_list, axis=2)]
  transfers between devices with their start and end apart: 11 -> 0, of which waited for: 8 -> 0; matrix products, arithmetic and copies ran while one was open for 52% -> 0% of each run, Pallas kernels for 0% -> 0%
where the time goes in v1:
time: 125 us
  Pallas kernels  122 us (98%)
  local copies, waits for them, and re-layouts  3.16 us (3%)
    pallas_call x1, Pallas kernels, shards(): pl.pallas_call(body, name='branch', out_shape=jax.ShapeDtypeStruct((1, 51...  122 us
    unnamed x1, local copies, waits for them, and re-layouts  3.16 us

profile of v1, /device:TPU:1, one launch (start us, length us, event | category | flops | bytes accessed | tf_op | source)
XLA Modules:
  0.0 125.1 jit_solution(15147017462288931934)
XLA Ops:
  0.0 122.0 %branch.1 = bf16[1,512,2048]{2,1,0:T(8,128)(2,1)} custom-call(bf16[1,512,4096]{2,1,0:T(8,128)(2,1)} %tokens.1, f32[1,4096]{1,0:T(1,128)} %bitcast.3, bf16[32,2048]{1,0:T(8,128)(2,1)} %lru.1, bf16[32,2048]{1,0:T(8,128)(2,1)} %gelu.1, f32[4,2048]{1,0:T(4,128)} %conv_w.1, f32[1,2048]{1,0:T(1,128)} %bitcast.4, bf16[256,512]{1,0:T(8,128)(2,1)} %gates.1, ...), custom_call_target="tpu_custom_call" | custom-call | tf_op jit(solution)/shard_map/branch/pallas_call | solution.py:493
  122.0 3.2 %copy.11 = bf16[1,512,2048]{2,1,0:T(8,128)(2,1)} copy(bf16[1,512,2048]{2,1,0:T(8,128)(2,1)} %branch.1) | data formatting | bytes 4194304

commit v2 on v1

--- a/solution.py
+++ b/solution.py
@@ -19,6 +19,10 @@
     (slice(16, 64), slice(0, 128)),
     (slice(16, 64), slice(128, 256)),
 )
+SEQUENCE = ((0, 0), (0, 1), (1, 0), (0, 2), (1, 1), (0, 3), (1, 2), (1, 3))
+LRU_AT = tuple(SEQUENCE.index((0, head)) for head in range(HEADS))
+GELU_AT = tuple(SEQUENCE.index((1, head)) for head in range(HEADS))
+GROUPS = ((0, 2), (2, 6))
 L_ROWS = 208
 T_ROWS = 128
 G_ROWS = 256
@@ -58,9 +62,6 @@
 
     def block(self, by, half=None):
         chunks = self.chunks
-        if self.phase == 0 and half is not None:
-            chunks = pl.ds(4 * half, 4)
-            half = None
         return piece(self.w, chunks, self.colour, self.phase, moved(self.coords, self.dim, by), half)
 
     def copy(self, hop, side, outgoing):
@@ -137,9 +138,9 @@
 
 def body(
     tokens, gain, lru, gelu, conv_w, conv_b, gates, gate_b, decay_p, out,
-    xn, w, gate_v, rec, local, cumul, outs, ends,
-    own_sem, p1_send, p1_recv, p2_send, p2_recv, p3_send, p3_recv,
-    tok_sem, halo_sem, gate_send, gate_recv, end_send, end_recv, out_sem, out_recv,
+    xn, w, stage, gate_v, rec, local, cumul, outs, ends,
+    own_sem, p1_send, p1_recv, pair_recv, p2_send, p2_recv, p3_send, p3_recv,
+    tok_sem, halo_sem, gate_send, gate_recv, pass_send, end_send, end_recv, out_sem, out_recv,
 ):
     fsdp = lax.axis_index("fsdp")
     seq = lax.axis_index("seq")
@@ -149,68 +150,105 @@
     coords = [x, y, z]
     partner = (fsdp, z * 2 + other)
 
+    def device(dim, by, on):
+        nx, ny, nz = moved(coords, dim, by)
+        return (nx * 4 + ny, nz * 2 + on)
+
     barrier = pltpu.get_barrier_semaphore()
-    for dim in (X, Y):
-        for by in (1, -1):
-            nx, ny, nz = moved(coords, dim, by)
-            pl.semaphore_signal(
-                barrier, inc=1, device_id=(nx * 4 + ny, nz * 2 + core), device_id_type=MESH
+    pl.semaphore_signal(barrier, inc=1, device_id=partner, device_id_type=MESH)
+    for dim in (X, Y, Z):
+        for by in (1, 2, 3):
+            for on in range(2):
+                pl.semaphore_signal(
+                    barrier, inc=1, device_id=device(dim, by, on), device_id_type=MESH
+                )
+
+    my_part = pl.ds(pl.multiple_of(core * 32, 32), 32)
+    own_copies = []
+    for n, (mat, head) in enumerate(SEQUENCE):
+        source = (lru, gelu)[mat]
+        for mine in range(2):
+            side = core if mine else other
+            first = pl.multiple_of(side * (HEADS * BW) + head * BW, BW)
+            dst = w.at[n, x, y, z, my_part, :] if mine else stage.at[n]
+            own_copies.append(
+                pltpu.make_async_copy(source.at[:, pl.ds(first, BW)], dst, own_sem.at[mine, n])
             )
-    for by in range(1, 8):
-        pl.semaphore_signal(
-            barrier, inc=1, device_id=(fsdp, lax.rem(seq + by, 8)), device_id_type=MESH
-        )
-
-    def own_copies(mine):
-        found = []
-        for mat, source in enumerate((lru, gelu)):
-            for head in range(HEADS):
-                side = core if mine else other
-                first = pl.multiple_of(side * (HEADS * BW) + head * BW, BW)
-                found.append(
-                    (
-                        source.at[:, pl.ds(first, BW)],
-                        w.at[2 * head + mat, x, y, z, pl.ds(pl.multiple_of(core * 32, 32), 32), :],
-                        2 * head + mat,
-                    )
-                )
-        return found
-
-    local_copies = [
-        pltpu.make_async_copy(src, dst, own_sem.at[0, n]) for src, dst, n in own_copies(True)
-    ]
-    for copy in local_copies:
+    for copy in own_copies:
         copy.start()
     my_rows = pl.ds(pl.multiple_of(HALO + core * 512, 16), 512)
     my_tokens = pltpu.make_async_copy(tokens.at[0], xn.at[my_rows, :], tok_sem.at[0])
     my_tokens.start()
-
-    pl.semaphore_wait(barrier, 11)
-
-    far_copies = [
+    for copy in own_copies:
+        copy.wait()
+
+    pl.semaphore_wait(barrier, 19)
+
+    def first_phase(group, colour, rows):
+        low, count = GROUPS[group]
+        chunks = pl.ds(low, count)
+        cols = pl.ds(PIECES[colour][1].start, PIECES[colour][1].stop - PIECES[colour][1].start)
+        land = pl.ds(pl.multiple_of(core * 32 + rows.start, 16), rows.stop - rows.start)
+        dst = w.at[chunks, x, y, z, land, cols]
+        for by in (1, 3, 2):
+            for on, src in (
+                (core, dst),
+                (other, stage.at[chunks, pl.ds(rows.start, rows.stop - rows.start), cols]),
+            ):
+                pltpu.make_async_remote_copy(
+                    src_ref=src,
+                    dst_ref=dst,
+                    send_sem=p1_send,
+                    recv_sem=p1_recv.at[group, colour],
+                    device_id=device(ORDERS[colour][0], by, on),
+                    device_id_type=MESH,
+                ).start()
+
+    def pair_phase(group):
+        low, count = GROUPS[group]
+        chunks = pl.ds(low, count)
         pltpu.make_async_remote_copy(
-            src_ref=src,
-            dst_ref=dst,
-            send_sem=own_sem.at[1, n],
-            recv_sem=own_sem.at[2, n],
+            src_ref=stage.at[chunks],
+            dst_ref=w.at[chunks, x, y, z, my_part, :],
+            send_sem=p1_send,
+            recv_sem=pair_recv.at[group],
             device_id=partner,
             device_id_type=MESH,
-        )
-        for src, dst, n in own_copies(False)
-    ]
-    for copy in far_copies:
-        copy.start()
-    for n, copy in enumerate(local_copies):
-        copy.wait()
-    other_rows = pl.ds(pl.multiple_of(other * 32, 32), 32)
-    for n in range(CHUNKS):
-        landed = w.at[n, x, y, z, other_rows, :]
-        pltpu.make_async_copy(landed, landed, own_sem.at[2, n]).wait()
+        ).start()
+
+    def first_start(group):
+        @pl.when(core == 0)
+        def _():
+            first_phase(group, 1, slice(16, 32))
+            first_phase(group, 2, slice(16, 32))
+            first_phase(group, 0, slice(0, 16))
+
+        @pl.when(core == 1)
+        def _():
+            first_phase(group, 1, slice(0, 32))
+            first_phase(group, 2, slice(0, 32))
+
+        pair_phase(group)
+
+    def first_wait(group):
+        low, count = GROUPS[group]
+        chunks = pl.ds(low, count)
+        landed = w.at[chunks, x, y, z, my_part, :]
+        pltpu.make_async_copy(landed, landed, pair_recv.at[group]).wait()
+        for colour in range(3):
+            at = [chunks, x, y, z]
+            at[1 + ORDERS[colour][0]] = pl.ds(0, 3)
+            rows, cols = PIECES[colour]
+            at.append(pl.ds(rows.start, rows.stop - rows.start))
+            at.append(pl.ds(cols.start, cols.stop - cols.start))
+            landed = w.at[tuple(at)]
+            pltpu.make_async_copy(landed, landed, p1_recv.at[group, colour]).wait()
+
+    first_start(0)
+    first_start(1)
 
     def ring(phase, n, colour):
-        send, recv = ((p1_send, p1_recv), (p2_send, p2_recv), (p3_send, p3_recv))[phase]
-        if phase == 0:
-            return Ring(w, pl.ds(0, CHUNKS), colour, 0, coords, core, send.at[colour], recv.at[colour])
+        send, recv = (None, (p2_send, p2_recv), (p3_send, p3_recv))[phase]
         return Ring(w, n, colour, phase, coords, core, send.at[colour], recv.at[n, colour])
 
     def start(phase, n, hop):
@@ -220,8 +258,6 @@
     def wait(phase, n, hop):
         for colour in range(3):
             ring(phase, n, colour).wait(hop)
-
-    start(0, None, 0)
 
     give_tokens = pltpu.make_async_remote_copy(
         src_ref=tokens.at[0],
@@ -248,9 +284,6 @@
         halo_copy(0).start()
         halo_copy(1).start()
 
-    wait(0, None, 0)
-    start(0, None, 1)
-
     kind = z // 2
     slot = (z % 2) * 2 + core
 
@@ -259,37 +292,76 @@
             src_ref=gates,
             dst_ref=gate_v.at[slot],
             send_sem=gate_send.at[by],
-            recv_sem=gate_recv.at[slot],
-            device_id=(fsdp, lax.rem(z + by, 4) * 2 + kind),
+            recv_sem=gate_recv.at[slot, 0],
+            device_id=device(Z, (0, 1, -1)[by], kind),
             device_id_type=MESH,
         )
 
     def gate_local():
-        return pltpu.make_async_copy(gates, gate_v.at[slot], gate_recv.at[slot])
-
-    @pl.when(core == kind)
-    def _():
-        gate_local().start()
-
-    @pl.when(core != kind)
-    def _():
-        gate_copy(0).start()
-
-    wait(0, None, 1)
-    start(1, 0, 0)
-    start(1, 1, 0)
-    start(1, 2, 0)
-    for by in range(1, 4):
-        gate_copy(by).start()
-
-    my_tokens.wait()
-    give_tokens.wait_recv()
-    halo_copy(0).wait_recv()
-
-    wait(1, 0, 0)
-    start(1, 0, 1)
-    wait(1, 1, 0)
-    start(1, 1, 1)
+        return pltpu.make_async_copy(gates, gate_v.at[slot], gate_recv.at[slot, 0])
+
+    def gate_start():
+        gate_copy(1).start()
+        gate_copy(2).start()
+
+        @pl.when(core == kind)
+        def _():
+            gate_local().start()
+
+        @pl.when(core != kind)
+        def _():
+            gate_copy(0).start()
+
+    def gate_half(j, half):
+        return gate_v.at[j, pl.ds(128 * half, 128), :]
+
+    def gate_pass(j, half):
+        return pltpu.make_async_remote_copy(
+            src_ref=gate_half(j, half),
+            dst_ref=gate_half(j, half),
+            send_sem=pass_send.at[j],
+            recv_sem=gate_recv.at[j, half],
+            device_id=device(Z, 1 - 2 * half, core),
+            device_id_type=MESH,
+        )
+
+    def landed(ref, sem):
+        pltpu.make_async_copy(ref, ref, sem).wait()
+
+    def gate_each(act):
+        for j in range(HEADS):
+            away = (z + 8 - (2 * core + j // 2)) % 4
+            act(j, away)
+
+    def gate_forward(j, away):
+        @pl.when(away == 0)
+        def _():
+            landed(gate_v.at[j], gate_recv.at[j, 0])
+
+        @pl.when(away == 1)
+        def _():
+            landed(gate_v.at[j], gate_recv.at[j, 0])
+            gate_pass(j, 0).start()
+
+        @pl.when(away == 3)
+        def _():
+            landed(gate_v.at[j], gate_recv.at[j, 0])
+            gate_pass(j, 1).start()
+
+    def gate_end(j, away):
+        @pl.when(away == 2)
+        def _():
+            landed(gate_half(j, 0), gate_recv.at[j, 0])
+            landed(gate_half(j, 1), gate_recv.at[j, 1])
+
+    def gate_drain(j, away):
+        @pl.when(away == 1)
+        def _():
+            gate_pass(j, 0).wait_send()
+
+        @pl.when(away == 3)
+        def _():
+            gate_pass(j, 1).wait_send()
 
     def norm_tile(i, _):
         rows = pl.ds(pl.multiple_of(i * 16, 16), 16)
@@ -303,19 +375,49 @@
     def norm(first, last):
         lax.fori_loop(first, last, norm_tile, 0)
 
-    norm(0, 20)
-    wait(1, 0, 1)
-    start(2, 0, 0)
-    wait(1, 2, 0)
-    start(1, 2, 1)
-    start(1, 3, 0)
-    norm(20, 65)
+    def p2_start(n):
+        start(1, n, 0)
+
+    def p2_pass(n):
+        wait(1, n, 0)
+        start(1, n, 1)
+
+    def p3_start(n):
+        wait(1, n, 1)
+        start(2, n, 0)
+
+    def p3_pass(n):
+        wait(2, n, 0)
+        start(2, n, 1)
+
+    first_wait(0)
+    p2_start(0)
+    p2_start(1)
+    first_wait(1)
+    for n in (2, 3, 4):
+        p2_start(n)
+    my_tokens.wait()
+    mine = 1 + core * 32
+    norm(mine, mine + 32)
+    for n in range(5):
+        p2_pass(n)
+    gate_start()
+    give_tokens.wait_recv()
+    halo_copy(0).wait_recv()
+    p3_start(0)
+    theirs = 1 + other * 32
+    norm(theirs, theirs + 32)
+    norm(0, 1)
+    p3_start(1)
+    gate_each(gate_forward)
+    p3_pass(0)
+    p3_start(2)
 
     def columns(head):
         return pl.ds(pl.multiple_of(core * (HEADS * BW) + head * BW, BW), BW)
 
-    def lru_chunk(head):
-        n = 2 * head
+    def lru_chunk(head, between):
+        n = LRU_AT[head]
 
         def rows_of(i, _):
             rows = pl.ds(pl.multiple_of(i * L_ROWS, 16), L_ROWS)
@@ -326,6 +428,7 @@
             return 0
 
         lax.fori_loop(0, (HALO + ROWS) // L_ROWS, rows_of, 0)
+        between()
         cols = columns(head)
         taps = conv_w[:, cols]
         bias = conv_b[:, cols]
@@ -377,8 +480,7 @@
 
     def end_landed(head, by):
         source = lax.rem(z + 4 - by, 4)
-        landed = ends.at[head, source]
-        pltpu.make_async_copy(landed, landed, end_recv.at[head, by - 1]).wait()
+        landed(ends.at[head, source], end_recv.at[head, by - 1])
 
     def out_copy(head, i, far):
         side = other if far else core
@@ -396,7 +498,7 @@
         return pltpu.make_async_copy(src, dst, out_sem.at[0, head, i])
 
     def gelu_chunk(head):
-        n = 2 * head + 1
+        n = GELU_AT[head]
         for by in range(1, 4):
             end_landed(head, by)
         begin = jnp.zeros((8, BW), jnp.float32)
@@ -422,49 +524,34 @@
                 outs[head, rows, :] = (state * part).astype(jnp.bfloat16)
                 out_copy(head, i, far).start()
 
-    for j in range(4):
-        landed = gate_v.at[j]
-        if j == 0:
-            pass
-
-    def compute(n):
-        head = n // 2
-        if n == 0:
-            for j in range(HEADS):
-                pltpu.make_async_copy(gate_v.at[j], gate_v.at[j], gate_recv.at[j]).wait()
-        if n % 2 == 0:
-            lru_chunk(head)
+    def before(n):
+        if n + 1 < CHUNKS:
+            p3_pass(n + 1)
+        if n + 3 < CHUNKS:
+            p3_start(n + 3)
+        if n + 5 < CHUNKS:
+            p2_start(n + 5)
+        if n >= 1 and n + 4 < CHUNKS:
+            p2_pass(n + 4)
+        wait(2, n, 1)
+
+    for n, (mat, head) in enumerate(SEQUENCE):
+        before(n)
+        if mat == 0:
+            lru_chunk(head, (lambda: gate_each(gate_end)) if n == 0 else (lambda: None))
             for by in range(1, 4):
                 end_copy(head, by).start()
         else:
             gelu_chunk(head)
 
-    for k in range(CHUNKS + 1):
-        if k + 1 < CHUNKS:
-            wait(1, k + 1, 1)
-            start(2, k + 1, 0)
-        if k < CHUNKS:
-            wait(2, k, 0)
-            start(2, k, 1)
-        if k + 4 < CHUNKS:
-            start(1, k + 4, 0)
-        if k + 3 < CHUNKS:
-            wait(1, k + 3, 0)
-            start(1, k + 3, 1)
-        if k >= 1:
-            wait(2, k - 1, 1)
-            compute(k - 1)
-
     for head in range(HEADS):
         for i in range(2):
             out_copy(head, i, False).wait()
             out_copy(head, i, True).wait_send()
-            landed = out.at[0, pl.ds(i * G_ROWS, G_ROWS), pl.ds(pl.multiple_of(other * (HEADS * BW) + head * BW, BW), BW)]
-            pltpu.make_async_copy(landed, landed, out_recv.at[head, i]).wait()
+            first = pl.multiple_of(other * (HEADS * BW) + head * BW, BW)
+            landed(out.at[0, pl.ds(i * G_ROWS, G_ROWS), pl.ds(first, BW)], out_recv.at[head, i])
         for by in range(1, 4):
             end_copy(head, by).wait_send()
-    for copy in far_copies:
-        copy.wait_send()
     give_tokens.wait_send()
 
     @pl.when(core == 1)
@@ -476,10 +563,12 @@
     def _():
         gate_copy(0).wait_send()
 
-    for by in range(1, 4):
-        gate_copy(by).wait_send()
-    for phase in range(3):
-        send = (p1_send, p2_send, p3_send)[phase]
+    gate_copy(1).wait_send()
+    gate_copy(2).wait_send()
+    gate_each(gate_drain)
+    sent = w.at[pl.ds(0, 7), x, y]
+    pltpu.make_async_copy(sent, sent, p1_send).wait()
+    for phase, send in ((1, p2_send), (2, p3_send)):
         for colour in range(3):
             every = Ring(w, pl.ds(0, CHUNKS), colour, phase, coords, core, send.at[colour], send.at[colour])
             for hop in range(2):
@@ -499,23 +588,26 @@
         scratch_shapes=[
             pltpu.VMEM((HALO + ROWS, WIDTH), jnp.bfloat16),
             pltpu.VMEM((CHUNKS, 4, 4, 4, 64, BW), jnp.bfloat16),
+            pltpu.VMEM((CHUNKS, 32, BW), jnp.bfloat16),
             pltpu.VMEM((HEADS, BW, 2 * BW), jnp.bfloat16),
             pltpu.VMEM((HALO + ROWS, BW), jnp.float32),
             pltpu.VMEM((2, ROWS, BW), jnp.float32),
             pltpu.VMEM((2, ROWS, BW), jnp.float32),
             pltpu.VMEM((HEADS, ROWS, BW), jnp.bfloat16),
             pltpu.VMEM((HEADS, 4, 2, 8, BW), jnp.float32),
-            dma((3, CHUNKS)),
-            dma((3, 2, 2)),
-            dma((3, 2, 2)),
+            dma((2, CHUNKS)),
+            dma,
+            dma((2, 3)),
+            dma((2,)),
             dma((3, 2, 2)),
             dma((CHUNKS, 3, 2, 2)),
             dma((3, 2, 2)),
             dma((CHUNKS, 3, 2, 2)),
             dma((3,)),
             dma((3,)),
-            dma((4,)),
-            dma((4,)),
+            dma((3,)),
+            dma((HEADS, 2)),
+            dma((HEADS,)),
             dma((HEADS, 3)),
             dma((HEADS, 3)),
             dma((2, HEADS, 2)),

time: 125 us -> 107 us (0.86)
  Pallas kernels: 122 us -> 104 us
    pallas_call x1, Pallas kernels: 122 us -> 104 us  [shards(): pl.pallas_call(body, name='branch', out_shape=jax.ShapeDtypeStruct((1, 51...]
where the time goes in v2:
time: 107 us
  Pallas kernels  104 us (97%)
  local copies, waits for them, and re-layouts  3.16 us (3%)
    pallas_call x1, Pallas kernels, shards(): pl.pallas_call(body, name='branch', out_shape=jax.ShapeDtypeStruct((1, 51...  104 us
    unnamed x1, local copies, waits for them, and re-layouts  3.16 us

profile of v2, /device:TPU:1, one launch (start us, length us, event | category | flops | bytes accessed | tf_op | source)
XLA Modules:
  0.0 106.7 jit_solution(17552829511923908913)
XLA Ops:
  0.0 103.5 %branch.1 = bf16[1,512,2048]{2,1,0:T(8,128)(2,1)} custom-call(bf16[1,512,4096]{2,1,0:T(8,128)(2,1)} %tokens.1, f32[1,4096]{1,0:T(1,128)} %bitcast.3, bf16[32,2048]{1,0:T(8,128)(2,1)} %lru.1, bf16[32,2048]{1,0:T(8,128)(2,1)} %gelu.1, f32[4,2048]{1,0:T(4,128)} %conv_w.1, f32[1,2048]{1,0:T(1,128)} %bitcast.4, bf16[256,512]{1,0:T(8,128)(2,1)} %gates.1, ...), custom_call_target="tpu_custom_call" | custom-call | tf_op jit(solution)/shard_map/branch/pallas_call | solution.py:582
  103.5 3.2 %copy.11 = bf16[1,512,2048]{2,1,0:T(8,128)(2,1)} copy(bf16[1,512,2048]{2,1,0:T(8,128)(2,1)} %branch.1) | data formatting | bytes 4194304

commit v3 on v2

v3 whole, which is shorter than its diff:
```python
import jax
import jax.numpy as jnp
from jax import lax
from jax.experimental import pallas as pl
from jax.experimental.pallas import tpu as pltpu
from jax.sharding import PartitionSpec as P

MESH = pl.DeviceIdType.MESH
HALO = 16
ROWS = 1024
WIDTH = 4096
HEADS = 4
BW = 256
CHUNKS = 8
X, Y, Z = 0, 1, 2
USUAL = ((X, Y, Z), (Y, Z, X), (Z, X, Y))
LATE = ((X, Y, Z), (Y, Z, X), (X, Z, Y))
PIECES = (
    (slice(0, 16), slice(0, 256)),
    (slice(16, 64), slice(0, 128)),
    (slice(16, 64), slice(128, 256)),
)
SEQUENCE = ((0, 0), (0, 1), (0, 2), (1, 0), (0, 3), (1, 1), (1, 2), (1, 3))
LRU_AT = tuple(SEQUENCE.index((0, head)) for head in range(HEADS))
GELU_AT = tuple(SEQUENCE.index((1, head)) for head in range(HEADS))
GROUPS = ((0, 2, USUAL), (2, 4, USUAL), (6, 2, LATE))
PLAN = (
    ("2s", 0), ("h",), ("2s", 1), ("1p", 2), ("2f", 0), ("g0",), ("no", 0), ("no", 1), ("2f", 1), ("2s", 3),
    ("3s", 0), ("1p", 6), ("2s", 2), ("3s", 1), ("2f", 2), ("2s", 4), ("3f", 0), ("g1",), ("2s", 5), ("no", 2),
    ("no", 3), ("2f", 3), ("3f", 1), ("2s", 6), ("nt", 0), ("nt", 1), ("nt", 2), ("2f", 4), ("3s", 2),
    ("nt", 3), ("3s", 3), ("hf",), ("2f", 6), ("nh",), ("2s", 7), ("2f", 5), ("3s", 4), ("L1", 0), ("3f", 2),
    ("L2", 0), ("3f", 3), ("L1", 1), ("3s", 5), ("L2", 1), ("2f", 7), ("3f", 4), ("L1", 2), ("3s", 6),
    ("L2", 2), ("3f", 5), ("G", 3), ("3s", 7), ("L1", 4), ("3f", 6), ("L2", 4), ("G", 5), ("3f", 7), ("G", 6),
    ("G", 7),
)
ORDERS = tuple(order for _, count, order in GROUPS for _ in range(count))
NORM = 2
T_ROWS = 128


def piece(w, chunks, order, colour, phase, coords, half=None):
    at = [chunks, None, None, None]
    for place, dim in enumerate(order):
        if place < phase:
            at[1 + dim] = pl.ds(0, 4)
            if place == 0 and half is not None:
                at[1 + dim] = pl.ds(2 * half, 2)
        else:
            at[1 + dim] = coords[dim]
    rows, cols = PIECES[colour]
    at.append(pl.ds(rows.start, rows.stop - rows.start))
    at.append(pl.ds(cols.start, cols.stop - cols.start))
    return w.at[tuple(at)]


def moved(coords, dim, by):
    new = list(coords)
    new[dim] = lax.rem(coords[dim] + (by + 4), 4)
    return new


class Ring:
    def __init__(self, w, chunks, order, colour, phase, coords, core, send, recv):
        self.w, self.chunks, self.colour, self.phase = w, chunks, colour, phase
        self.coords, self.core, self.send, self.recv = coords, core, send, recv
        self.order = order
        self.dim = order[phase]

    def device(self, by):
        x, y, z = moved(self.coords, self.dim, by)
        return (x * 4 + y, z * 2 + self.core)

    def block(self, by, half=None):
        chunks = self.chunks
        return piece(self.w, chunks, self.order, self.colour, self.phase, moved(self.coords, self.dim, by), half)

    def start(self, hop, sides=(0, 1)):
        for side in sides:
            way = 1 - 2 * side
            ref = self.block(-way * hop, None if hop == 0 or self.phase == 0 else side)
            pltpu.make_async_remote_copy(
                src_ref=ref,
                dst_ref=ref,
                send_sem=self.send,
                recv_sem=self.recv,
                device_id=self.device(way),
                device_id_type=MESH,
            ).start()


def softplus_of(value):
    small = jnp.exp(-jnp.abs(value))
    ratio = small / (2.0 + small)
    square = ratio * ratio
    series = jnp.full_like(value, 1.0 / 17.0)
    for divisor in (15.0, 13.0, 11.0, 9.0, 7.0, 5.0, 3.0, 1.0):
        series = series * square + 1.0 / divisor
    return jnp.maximum(value, 0.0) + 2.0 * ratio * series


def one_minus_square(decay, twice):
    return jnp.tanh(-0.5 * twice) * (1.0 + decay * decay)


def root(value):
    return value * lax.rsqrt(jnp.maximum(value, 1e-37))


def tile_scan(decay, driven, carry_a, carry_b):
    rows, cols = decay.shape
    groups = rows // 8
    group = decay.reshape(groups, 8, cols)
    state = driven.reshape(groups, 8, cols)
    place = lax.broadcasted_iota(jnp.int32, (1, 8, cols), 1)
    for step in (1, 2, 4):
        inside = place >= step
        a_prev = jnp.where(inside, pltpu.roll(group, step, 1), 1.0)
        b_prev = jnp.where(inside, pltpu.roll(state, step, 1), 0.0)
        state = group * b_prev + state
        group = group * a_prev
    last_a = jnp.broadcast_to(group[:, 7:8, :], group.shape)
    last_b = jnp.broadcast_to(state[:, 7:8, :], state.shape)
    products, states = [], []
    for g in range(groups):
        products.append(group[g] * carry_a)
        states.append(state[g] + group[g] * carry_b)
        carry_b = last_b[g] + last_a[g] * carry_b
        carry_a = last_a[g] * carry_a
    return jnp.concatenate(products, 0), jnp.concatenate(states, 0), carry_a, carry_b


def body(
    tokens, gain, lru, gelu, conv_w, conv_b, gates, gate_b, decay_p, out,
    xn, w, stage, gate_own, gate_v, rec, local, cumul, outs, ends,
    own_sem, p1_send, p1_recv, pass_recv, pair_recv, p2_send, p2_recv, p3_send, p3_recv,
    tok_sem, halo_sem, gate_send, gate_recv, pass_send, end_send, end_recv, out_sem, out_recv,
):
    fsdp = lax.axis_index("fsdp")
    seq = lax.axis_index("seq")
    x, y = fsdp // 4, fsdp % 4
    z, core = seq // 2, seq % 2
    other = 1 - core
    coords = [x, y, z]
    partner = (fsdp, z * 2 + other)

    def device(dim, by, on):
        nx, ny, nz = moved(coords, dim, by)
        return (nx * 4 + ny, nz * 2 + on)

    barrier = pltpu.get_barrier_semaphore()
    pl.semaphore_signal(barrier, inc=1, device_id=partner, device_id_type=MESH)
    for dim in (X, Y, Z):
        for by in (1, 2, 3):
            for on in range(2):
                pl.semaphore_signal(
                    barrier, inc=1, device_id=device(dim, by, on), device_id_type=MESH
                )

    my_part = pl.ds(pl.multiple_of(core * 32, 32), 32)
    own_copies = []
    for n, (mat, head) in enumerate(SEQUENCE):
        source = (lru, gelu)[mat]
        for mine in range(2):
            side = core if mine else other
            first = pl.multiple_of(side * (HEADS * BW) + head * BW, BW)
            dst = w.at[n, x, y, z, my_part, :] if mine else stage.at[n]
            own_copies.append(
                pltpu.make_async_copy(source.at[:, pl.ds(first, BW)], dst, own_sem)
            )
    for copy in own_copies:
        copy.start()
    xn[pl.ds(0, HALO), :] = jnp.zeros((HALO, WIDTH), jnp.bfloat16)
    my_rows = pl.ds(pl.multiple_of(HALO + core * 512, 16), 512)
    my_tokens = pltpu.make_async_copy(tokens.at[0], xn.at[my_rows, :], tok_sem.at[0])
    my_tokens.start()
    stage_gate = pltpu.make_async_copy(gates, gate_own, gate_send.at[3])
    stage_gate.start()
    pltpu.make_async_copy(w.at[0, x, pl.ds(0, 2)], w.at[0, x, pl.ds(0, 2)], own_sem).wait()

    pl.semaphore_wait(barrier, 19)

    def landed(ref, sem):
        pltpu.make_async_copy(ref, ref, sem).wait()

    def first_phase(group, colour, rows):
        low, count, order = GROUPS[group]
        chunks = pl.ds(low, count)
        cols = pl.ds(PIECES[colour][1].start, PIECES[colour][1].stop - PIECES[colour][1].start)
        land = pl.ds(pl.multiple_of(core * 32 + rows.start, 16), rows.stop - rows.start)
        dst = w.at[chunks, x, y, z, land, cols]
        for by in (1, 3, 2) if group == 0 else (1, 3):
            for on, src in (
                (core, dst),
                (other, stage.at[chunks, pl.ds(rows.start, rows.stop - rows.start), cols]),
            ):
                pltpu.make_async_remote_copy(
                    src_ref=src,
                    dst_ref=dst,
                    send_sem=p1_send.at[min(group, 1)],
                    recv_sem=p1_recv.at[group],
                    device_id=device(order[colour][0], by, on),
                    device_id_type=MESH,
                ).start()

    def first_start(group):
        low, count, _ = GROUPS[group]
        chunks = pl.ds(low, count)

        @pl.when(core == 0)
        def _():
            first_phase(group, 1, slice(16, 32))
            first_phase(group, 2, slice(16, 32))
            first_phase(group, 0, slice(0, 16))

        @pl.when(core == 1)
        def _():
            first_phase(group, 1, slice(0, 32))
            first_phase(group, 2, slice(0, 32))

        pltpu.make_async_remote_copy(
            src_ref=stage.at[chunks],
            dst_ref=w.at[chunks, x, y, z, my_part, :],
            send_sem=p1_send.at[min(group, 1)],
            recv_sem=pair_recv.at[group],
            device_id=partner,
            device_id_type=MESH,
        ).start()

    def first_wait(group):
        low, count, _ = GROUPS[group]
        chips = 3 if group == 0 else 2
        landed(w.at[pl.ds(low, count), x, y, pl.ds(0, chips)], p1_recv.at[group])
        landed(w.at[pl.ds(low, count), x, y, z, my_part, :], pair_recv.at[group])

    def first_pass(group):
        low, count, order = GROUPS[group]
        half = count // 2
        for colour in range(3):
            for side in range(2):
                Ring(
                    w, pl.ds(low + half * side, half), order[colour], colour, 0, coords, core,
                    p1_send.at[2], pass_recv.at[group],
                ).start(1, (side,))

    def first_last(group):
        low, count, _ = GROUPS[group]
        landed(w.at[pl.ds(low, count), x, y, z], pass_recv.at[group])

    for group in range(3):
        first_start(group)

    def start(phase, n, hop):
        send, recv = (None, (p2_send, p2_recv), (p3_send, p3_recv))[phase]
        for colour in range(3):
            Ring(
                w, n, ORDERS[n][colour], colour, phase, coords, core, send, recv.at[n, hop]
            ).start(hop)

    def wait(phase, n, hop):
        if phase == 1:
            landed(w.at[n, x, pl.ds(0, 2 - hop)], p2_recv.at[n, hop])
        else:
            landed(w.at[n, pl.ds(0, 2 - hop)], p3_recv.at[n, hop])

    give_tokens = pltpu.make_async_remote_copy(
        src_ref=tokens.at[0],
        dst_ref=xn.at[my_rows, :],
        send_sem=tok_sem.at[1],
        recv_sem=tok_sem.at[2],
        device_id=partner,
        device_id_type=MESH,
    )

    halo_rows = xn.at[pl.ds(8, 8), :]

    def halo_out():
        return pltpu.make_async_remote_copy(
            src_ref=tokens.at[0, pl.ds(504, 8), :],
            dst_ref=halo_rows,
            send_sem=halo_sem.at[0],
            recv_sem=halo_sem.at[2],
            device_id=device(Z, 1, 1),
            device_id_type=MESH,
        )

    def halo_over():
        return pltpu.make_async_remote_copy(
            src_ref=halo_rows,
            dst_ref=halo_rows,
            send_sem=halo_sem.at[1],
            recv_sem=halo_sem.at[2],
            device_id=partner,
            device_id_type=MESH,
        )

    def halo_start():
        @pl.when(core == 1)
        def _():
            halo_out().start()

    def halo_pass():
        @pl.when(core == 1)
        def _():
            halo_out().wait_recv()
            halo_over().start()

    def halo_norm():
        @pl.when(core == 1)
        def _():
            halo_over().wait_send()

        @pl.when(core == 0)
        def _():
            halo_over().wait_recv()

        norm_rows(0, True)

    kind = z // 2
    slot = (z % 2) * 2 + core

    def gate_copy(by):
        return pltpu.make_async_remote_copy(
            src_ref=gate_own,
            dst_ref=gate_v.at[slot],
            send_sem=gate_send.at[by],
            recv_sem=gate_recv.at[slot, 0],
            device_id=device(Z, (0, 1, -1)[by], kind),
            device_id_type=MESH,
        )

    def gate_local():
        return pltpu.make_async_copy(gates, gate_v.at[slot], gate_recv.at[slot, 0])

    def gate_start():
        stage_gate.wait()
        gate_copy(1).start()
        gate_copy(2).start()

        @pl.when(core == kind)
        def _():
            gate_local().start()

        @pl.when(core != kind)
        def _():
            gate_copy(0).start()

    def gate_half(j, half):
        return gate_v.at[j, pl.ds(128 * half, 128), :]

    def gate_pass(j, half):
        return pltpu.make_async_remote_copy(
            src_ref=gate_half(j, half),
            dst_ref=gate_half(j, half),
            send_sem=pass_send.at[j],
            recv_sem=gate_recv.at[j, half],
            device_id=device(Z, 1 - 2 * half, core),
            device_id_type=MESH,
        )

    def gate_each(act):
        for j in range(HEADS):
            away = (z + 8 - (2 * core + j // 2)) % 4
            act(j, away)

    def gate_forward(j, away):
        @pl.when(away == 0)
        def _():
            landed(gate_v.at[j], gate_recv.at[j, 0])

        @pl.when(away == 1)
        def _():
            landed(gate_v.at[j], gate_recv.at[j, 0])
            gate_pass(j, 0).start()

        @pl.when(away == 3)
        def _():
            landed(gate_v.at[j], gate_recv.at[j, 0])
            gate_pass(j, 1).start()

    def gate_end(j, away):
        @pl.when(away == 2)
        def _():
            landed(gate_half(j, 0), gate_recv.at[j, 0])
            landed(gate_half(j, 1), gate_recv.at[j, 1])

    def gate_drain(j, away):
        @pl.when(away == 1)
        def _():
            gate_pass(j, 0).wait_send()

        @pl.when(away == 3)
        def _():
            gate_pass(j, 1).wait_send()

    def norm_rows(i, first):
        rows = pl.ds(pl.multiple_of(i * 16, 16), 16)
        value = xn[rows, :].astype(jnp.float32)
        mean = jnp.mean(value * value, axis=-1, keepdims=True)
        normed = value * lax.rsqrt(mean + 1e-06) * gain[...]
        if first:
            normed = normed * jnp.where(z == 0, 0.0, 1.0)
        xn[rows, :] = normed.astype(jnp.bfloat16)

    def norm(side, part):
        base = 1 + side * 32 + part * 8

        def pair(i, _):
            for k in range(NORM):
                norm_rows(base + i * NORM + k, False)
            return 0

        lax.fori_loop(0, 8 // NORM, pair, 0)

    def p2_start(n):
        start(1, n, 0)

    def p2_pass(n):
        wait(1, n, 0)
        start(1, n, 1)

    def p3_start(n):
        wait(1, n, 1)
        start(2, n, 0)

    def p3_pass(n):
        wait(2, n, 0)
        start(2, n, 1)

    def columns(head):
        return pl.ds(pl.multiple_of(core * (HEADS * BW) + head * BW, BW), BW)

    def lru_rows(head):
        n = LRU_AT[head]

        for low, high in ((0, 528), (528, HALO + ROWS)):
            value = jnp.dot(
                xn[low:high, :], w[n].reshape(WIDTH, BW), preferred_element_type=jnp.float32
            )
            rec[low:high, :] = value.astype(jnp.bfloat16).astype(jnp.float32)

    def lru_tiles(head):
        cols = columns(head)
        taps = conv_w[:, cols]
        bias = conv_b[:, cols]
        g_bias = gate_b[:, cols]
        rate = -8.0 * softplus_of(decay_p[:, cols])
        gate_block = gates_of(head)

        def tile(i, carry):
            carry_a, carry_b = carry
            first = pl.multiple_of(i * T_ROWS + (HALO - 8), 8)
            value = rec[pl.ds(first, T_ROWS + 8), :]
            total = jnp.zeros((T_ROWS, BW), jnp.float32) + bias
            for tap in range(4):
                total = total + taps[tap : tap + 1, :] * value[8 - tap : 8 - tap + T_ROWS, :]
            conv = total.astype(jnp.bfloat16)
            gate = jnp.dot(conv, gate_block, preferred_element_type=jnp.float32)
            input_gate = jax.nn.sigmoid(gate[:, :BW] + g_bias[0:1, :])
            recur_gate = jax.nn.sigmoid(gate[:, BW:] + g_bias[1:2, :])
            log_decay = rate * recur_gate
            decay = jnp.exp(log_decay)
            driven = (
                root(one_minus_square(decay, 2.0 * log_decay))
                * input_gate
                * conv.astype(jnp.float32)
            )
            rows = pl.ds(pl.multiple_of(i * T_ROWS, T_ROWS), T_ROWS)
            products, states, carry_a, carry_b = tile_scan(decay, driven, carry_a, carry_b)
            cumul[head, rows, :] = products
            local[head, rows, :] = states
            return carry_a, carry_b

        begin = (jnp.ones((8, BW), jnp.float32), jnp.zeros((8, BW), jnp.float32))
        end_a, end_b = lax.fori_loop(0, ROWS // T_ROWS, tile, begin)
        ends[head, z, 0, :, :] = end_a
        ends[head, z, 1, :, :] = end_b

    def gates_of(head):
        return gate_v[head]

    def end_copy(head, by):
        return pltpu.make_async_remote_copy(
            src_ref=ends.at[head, z],
            dst_ref=ends.at[head, z],
            send_sem=end_send,
            recv_sem=end_recv.at[head],
            device_id=(fsdp, lax.rem(z + by, 4) * 2 + core),
            device_id_type=MESH,
        )

    def ends_landed(head):
        landed(ends.at[head, pl.ds(0, 3)], end_recv.at[head])

    def out_copy(head):
        return pltpu.make_async_remote_copy(
            src_ref=outs.at[head],
            dst_ref=out.at[0, :, columns(head)],
            send_sem=out_sem,
            recv_sem=out_recv.at[head],
            device_id=partner,
            device_id_type=MESH,
        )

    def gelu_chunk(head):
        n = GELU_AT[head]
        ends_landed(head)
        begin = jnp.zeros((8, BW), jnp.float32)
        for source in range(3):
            after = ends[head, source, 0] * begin + ends[head, source, 1]
            begin = jnp.where(source < z, after, begin)
        def rows_of(side):
            first = pl.multiple_of(side * 512, 512)
            rec[pl.ds(first, 512), :] = jnp.dot(
                xn[pl.ds(pl.multiple_of(first + HALO, 16), 512), :],
                w[n].reshape(WIDTH, BW),
                preferred_element_type=jnp.float32,
            )

        start_state = begin[0:1, :]

        def part(i, side):
            rows = pl.ds(pl.multiple_of(side * 512 + i * T_ROWS, T_ROWS), T_ROWS)
            gelu_in = rec[rows, :]
            state = local[head, rows, :] + cumul[head, rows, :] * start_state
            inner = gelu_in * (
                0.7978845608028654 + (0.7978845608028654 * 0.044715) * (gelu_in * gelu_in)
            )
            gelu_out = 0.5 * gelu_in * (1.0 + jnp.tanh(inner))
            return (state * gelu_out).astype(jnp.bfloat16)

        def far_part(i, _):
            outs[head, pl.ds(pl.multiple_of(i * T_ROWS, T_ROWS), T_ROWS), :] = part(i, other)
            return 0

        def near_part(i, _):
            rows = pl.ds(pl.multiple_of(i * T_ROWS, T_ROWS), T_ROWS)
            out[0, rows, columns(head)] = part(i, core)
            return 0

        def half(i, _):
            rows_of((other + i) % 2)

            @pl.when(i == 0)
            def _():
                lax.fori_loop(0, 512 // T_ROWS, far_part, 0)
                out_copy(head).start()

            @pl.when(i == 1)
            def _():
                lax.fori_loop(0, 512 // T_ROWS, near_part, 0)

            return 0

        lax.fori_loop(0, 2, half, 0)

    def group_of(n):
        return [low + count > n for low, count, _ in GROUPS].index(True)

    waited = set()

    def once(what, act):
        if what not in waited:
            waited.add(what)
            act()

    def first_ready(group):
        if group == 0:
            first_wait(0)
        else:
            first_last(group)

    def step(kind, n=None):
        if kind == "1p":
            first_wait(group_of(n))
            first_pass(group_of(n))
        elif kind == "2s":
            once(("first", group_of(n)), lambda: first_ready(group_of(n)))
            p2_start(n)
            once("give", give_tokens.start)
        elif kind == "2f":
            p2_pass(n)
        elif kind == "3s":
            p3_start(n)
        elif kind == "3f":
            p3_pass(n)
        elif kind == "h":
            halo_start()
        elif kind == "hf":
            halo_pass()
        elif kind == "nh":
            halo_norm()
        elif kind == "g0":
            gate_start()
        elif kind == "g1":
            gate_each(gate_forward)
        elif kind == "no":
            once("mine", my_tokens.wait)
            norm(core, n)
        elif kind == "nt":
            once("theirs", give_tokens.wait_recv)
            norm(other, n)
        elif kind == "L1":
            wait(2, n, 1)
            lru_rows(SEQUENCE[n][1])
        elif kind == "L2":
            if n == 0:
                gate_each(gate_end)
            lru_tiles(SEQUENCE[n][1])
            for by in range(1, 4):
                end_copy(SEQUENCE[n][1], by).start()
        elif kind == "G":
            wait(2, n, 1)
            gelu_chunk(SEQUENCE[n][1])

    for what in PLAN:
        with jax.named_scope("s" + "_".join(str(item) for item in what)):
            step(*what)

    with jax.named_scope("outs"):
        for head in range(HEADS):
            first = pl.multiple_of(other * (HEADS * BW) + head * BW, BW)
            landed(out.at[0, :, pl.ds(first, BW)], out_recv.at[head])
    landed(outs, out_sem)
    landed(ends.at[:, pl.ds(0, 3)], end_send)
    with jax.named_scope("rest"):
        give_tokens.wait_send()

    @pl.when(core == 1)
    def _():
        halo_out().wait_send()

    @pl.when(core != kind)
    def _():
        gate_copy(0).wait_send()

    gate_copy(1).wait_send()
    gate_copy(2).wait_send()
    gate_each(gate_drain)
    landed(w.at[pl.ds(0, 7), x, y, z], p1_send.at[0])
    landed(w.at[pl.ds(0, 5), pl.ds(0, 3), y, z], p1_send.at[1])
    landed(w.at[pl.ds(0, 6), x, y, z], p1_send.at[2])
    landed(w.at[pl.ds(0, 3), pl.ds(0, 2)], p2_send)
    landed(w.at[pl.ds(0, 6)], p3_send)


def shards(tokens, norm_gain, lru, gelu, conv_weight, conv_bias, gates, gate_bias, decay_param):
    dma = pltpu.SemaphoreType.DMA
    hbm = pl.BlockSpec(memory_space=pl.ANY)
    vmem = pl.BlockSpec(memory_space=pltpu.VMEM)
    return pl.pallas_call(
        body,
        name="branch",
        out_shape=pltpu.VMEM((1, 512, 2048), jnp.bfloat16),
        in_specs=[hbm, vmem, hbm, hbm, vmem, vmem, hbm, vmem, vmem],
        out_specs=vmem,
        scratch_shapes=[
            pltpu.VMEM((HALO + ROWS, WIDTH), jnp.bfloat16),
            pltpu.VMEM((CHUNKS, 4, 4, 4, 64, BW), jnp.bfloat16),
            pltpu.VMEM((CHUNKS, 32, BW), jnp.bfloat16),
            pltpu.VMEM((BW, 2 * BW), jnp.bfloat16),
            pltpu.VMEM((HEADS, BW, 2 * BW), jnp.bfloat16),
            pltpu.VMEM((HALO + ROWS, BW), jnp.float32),
            pltpu.VMEM((HEADS, ROWS, BW), jnp.float32),
            pltpu.VMEM((HEADS, ROWS, BW), jnp.float32),
            pltpu.VMEM((HEADS, 512, BW), jnp.bfloat16),
            pltpu.VMEM((HEADS, 4, 2, 8, BW), jnp.float32),
            dma,
            dma((3,)),
            dma((3,)),
            dma((3,)),
            dma((3,)),
            dma,
            dma((CHUNKS, 2)),
            dma,
            dma((CHUNKS, 2)),
            dma((3,)),
            dma((3,)),
            dma((4,)),
            dma((HEADS, 2)),
            dma((HEADS,)),
            dma,
            dma((HEADS,)),
            dma,
            dma((HEADS,)),
        ],
        compiler_params=pltpu.CompilerParams(
            collective_id=0, has_side_effects=True, vmem_limit_bytes=56 * 1024 * 1024
        ),
    )(
        tokens,
        norm_gain.reshape(1, -1),
        lru,
        gelu,
        conv_weight,
        conv_bias.reshape(1, -1),
        gates,
        gate_bias,
        decay_param.reshape(1, -1),
    )


def solution(mesh):
    placed = (
        P("fsdp", "seq", None),
        P(),
        P(("fsdp", "seq"), None),
        P(("fsdp", "seq"), None),
        P(),
        P(),
        P("seq", None),
        P(),
        P(),
    )
    return jax.shard_map(
        shards, mesh=mesh, in_specs=placed, out_specs=P("fsdp", "seq", None), check_vma=False
    )
```

time: 107 us -> 87.5 us (0.82)
  Pallas kernels: 104 us -> 86 us
  local copies, waits for them, and re-layouts: 3.16 us -> 1.32 us
    pallas_call x1, Pallas kernels: 104 us -> 86 us  [shards(): pl.pallas_call(body, name='branch', out_shape=pltpu.VMEM((1, 512, 2048),...]
    unnamed x1, local copies, waits for them, and re-layouts: 3.16 us -> 1.32 us
where the time goes in v3:
time: 87.5 us; the launch traced here: 87.3 us
  Pallas kernels  86 us (98%)
  local copies, waits for them, and re-layouts  1.32 us (2%)
    pallas_call x1, Pallas kernels, shards(): pl.pallas_call(body, name='branch', out_shape=pltpu.VMEM((1, 512, 2048),...  86 us

profile of v3, /device:TPU:1, one launch (start us, length us, event | category | flops | bytes accessed | tf_op | source)
XLA Modules:
  0.0 87.3 jit_solution(10555373989901530461)
XLA Ops:
  0.0 86.0 %branch.1 = bf16[1,512,2048]{2,1,0:T(8,128)(2,1)S(1)} custom-call(bf16[1,512,4096]{2,1,0:T(8,128)(2,1)} %tokens.1, f32[1,4096]{1,0:T(1,128)} %bitcast.3, bf16[32,2048]{1,0:T(8,128)(2,1)} %lru.1, bf16[32,2048]{1,0:T(8,128)(2,1)} %gelu.1, f32[4,2048]{1,0:T(4,128)} %conv_w.1, f32[1,2048]{1,0:T(1,128)} %bitcast.4, bf16[256,512]{1,0:T(8,128)(2,1)} %gates.1, ...), custom_call_target="tpu_custom_call" | custom-call | tf_op jit(solution)/shard_map/branch/pallas_call | solution.py:650
  86.0 1.3 %copy.11 = bf16[1,512,2048]{2,1,0:T(8,128)(2,1)} copy(bf16[1,512,2048]{2,1,0:T(8,128)(2,1)S(1)} %branch.1) | data formatting | bytes 4194304

commit v4 on v3

--- a/solution.py
+++ b/solution.py
@@ -25,17 +25,17 @@
 GELU_AT = tuple(SEQUENCE.index((1, head)) for head in range(HEADS))
 GROUPS = ((0, 2, USUAL), (2, 4, USUAL), (6, 2, LATE))
 PLAN = (
-    ("2s", 0), ("h",), ("2s", 1), ("1p", 2), ("2f", 0), ("g0",), ("no", 0), ("no", 1), ("2f", 1), ("2s", 3),
-    ("3s", 0), ("1p", 6), ("2s", 2), ("3s", 1), ("2f", 2), ("2s", 4), ("3f", 0), ("g1",), ("2s", 5), ("no", 2),
-    ("no", 3), ("2f", 3), ("3f", 1), ("2s", 6), ("nt", 0), ("nt", 1), ("nt", 2), ("2f", 4), ("3s", 2),
-    ("nt", 3), ("3s", 3), ("hf",), ("2f", 6), ("nh",), ("2s", 7), ("2f", 5), ("3s", 4), ("L1", 0), ("3f", 2),
-    ("L2", 0), ("3f", 3), ("L1", 1), ("3s", 5), ("L2", 1), ("2f", 7), ("3f", 4), ("L1", 2), ("3s", 6),
-    ("L2", 2), ("3f", 5), ("G", 3), ("3s", 7), ("L1", 4), ("3f", 6), ("L2", 4), ("G", 5), ("3f", 7), ("G", 6),
-    ("G", 7),
+    ("t", 1), ("g0", 0), ("1p", 2), ("2s", 0), ("no", 0), ("2s", 1), ("1p", 6), ("h",), ("2s", 3), ("2s", 2),
+    ("2f", 0), ("t", 0), ("2s", 6), ("2s", 5), ("no", 1), ("2f", 1), ("2f", 3), ("2f", 2), ("hf",), ("2s", 4),
+    ("3s", 0), ("t", 2), ("no", 2), ("no", 3), ("3s", 1), ("g0", 1), ("2f", 4), ("3s", 2), ("nt", 0), ("3f", 0),
+    ("t", 3), ("g1", 1), ("g1", 0), ("3s", 3), ("2f", 5), ("2f", 6), ("3f", 1), ("3f", 2), ("nt", 1), ("3s", 4),
+    ("nt", 2), ("2s", 7), ("nt", 3), ("nh",), ("L1", 0), ("L2", 0), ("3s", 5), ("L1", 1), ("3f", 3), ("L2", 1),
+    ("3f", 4), ("L1", 2), ("2f", 7), ("3s", 6), ("L2", 2), ("3f", 5), ("G", 3), ("3s", 7), ("L1", 4), ("3f", 6),
+    ("L2", 4), ("G", 5), ("3f", 7), ("G", 6), ("G", 7),
 )
 ORDERS = tuple(order for _, count, order in GROUPS for _ in range(count))
-NORM = 2
-T_ROWS = 128
+NORM = 8
+T_ROWS = 256
 
 
 def piece(w, chunks, order, colour, phase, coords, half=None):
@@ -133,7 +133,7 @@
     tokens, gain, lru, gelu, conv_w, conv_b, gates, gate_b, decay_p, out,
     xn, w, stage, gate_own, gate_v, rec, local, cumul, outs, ends,
     own_sem, p1_send, p1_recv, pass_recv, pair_recv, p2_send, p2_recv, p3_send, p3_recv,
-    tok_sem, halo_sem, gate_send, gate_recv, pass_send, end_send, end_recv, out_sem, out_recv,
+    tok_sem, tok_recv, halo_sem, gate_send, gate_recv, pass_send, end_send, end_recv, out_sem, out_recv,
 ):
     fsdp = lax.axis_index("fsdp")
     seq = lax.axis_index("seq")
@@ -147,14 +147,8 @@
         nx, ny, nz = moved(coords, dim, by)
         return (nx * 4 + ny, nz * 2 + on)
 
-    barrier = pltpu.get_barrier_semaphore()
-    pl.semaphore_signal(barrier, inc=1, device_id=partner, device_id_type=MESH)
-    for dim in (X, Y, Z):
-        for by in (1, 2, 3):
-            for on in range(2):
-                pl.semaphore_signal(
-                    barrier, inc=1, device_id=device(dim, by, on), device_id_type=MESH
-                )
+    def group_at(n):
+        return [low + count > n for low, count, _ in GROUPS].index(True)
 
     my_part = pl.ds(pl.multiple_of(core * 32, 32), 32)
     own_copies = []
@@ -165,18 +159,27 @@
             first = pl.multiple_of(side * (HEADS * BW) + head * BW, BW)
             dst = w.at[n, x, y, z, my_part, :] if mine else stage.at[n]
             own_copies.append(
-                pltpu.make_async_copy(source.at[:, pl.ds(first, BW)], dst, own_sem)
+                pltpu.make_async_copy(source.at[:, pl.ds(first, BW)], dst, own_sem.at[group_at(n)])
             )
     for copy in own_copies:
         copy.start()
+
     xn[pl.ds(0, HALO), :] = jnp.zeros((HALO, WIDTH), jnp.bfloat16)
+
+    barrier = pltpu.get_barrier_semaphore()
+    pl.semaphore_signal(barrier, inc=1, device_id=partner, device_id_type=MESH)
+    for dim in (X, Y, Z):
+        for by in (1, 2, 3):
+            for on in range(2):
+                pl.semaphore_signal(
+                    barrier, inc=1, device_id=device(dim, by, on), device_id_type=MESH
+                )
+
     my_rows = pl.ds(pl.multiple_of(HALO + core * 512, 16), 512)
     my_tokens = pltpu.make_async_copy(tokens.at[0], xn.at[my_rows, :], tok_sem.at[0])
     my_tokens.start()
     stage_gate = pltpu.make_async_copy(gates, gate_own, gate_send.at[3])
     stage_gate.start()
-    pltpu.make_async_copy(w.at[0, x, pl.ds(0, 2)], w.at[0, x, pl.ds(0, 2)], own_sem).wait()
-
     pl.semaphore_wait(barrier, 19)
 
     def landed(ref, sem):
@@ -188,7 +191,7 @@
         cols = pl.ds(PIECES[colour][1].start, PIECES[colour][1].stop - PIECES[colour][1].start)
         land = pl.ds(pl.multiple_of(core * 32 + rows.start, 16), rows.stop - rows.start)
         dst = w.at[chunks, x, y, z, land, cols]
-        for by in (1, 3, 2) if group == 0 else (1, 3):
+        for by in (2, 1, 3) if group == 0 else (1, 3):
             for on, src in (
                 (core, dst),
                 (other, stage.at[chunks, pl.ds(rows.start, rows.stop - rows.start), cols]),
@@ -247,6 +250,8 @@
         landed(w.at[pl.ds(low, count), x, y, z], pass_recv.at[group])
 
     for group in range(3):
+        pair = w.at[pl.ds(0, GROUPS[group][1]), x, y, z]
+        landed(pair, own_sem.at[group])
         first_start(group)
 
     def start(phase, n, hop):
@@ -262,14 +267,15 @@
         else:
             landed(w.at[n, pl.ds(0, 2 - hop)], p3_recv.at[n, hop])
 
-    give_tokens = pltpu.make_async_remote_copy(
-        src_ref=tokens.at[0],
-        dst_ref=xn.at[my_rows, :],
-        send_sem=tok_sem.at[1],
-        recv_sem=tok_sem.at[2],
-        device_id=partner,
-        device_id_type=MESH,
-    )
+    def give_tokens(i):
+        return pltpu.make_async_remote_copy(
+            src_ref=tokens.at[0, pl.ds(i * 128, 128), :],
+            dst_ref=xn.at[pl.ds(pl.multiple_of(HALO + core * 512 + i * 128, 16), 128), :],
+            send_sem=tok_sem.at[1],
+            recv_sem=tok_recv.at[i],
+            device_id=partner,
+            device_id_type=MESH,
+        )
 
     halo_rows = xn.at[pl.ds(8, 8), :]
 
@@ -318,39 +324,40 @@
     kind = z // 2
     slot = (z % 2) * 2 + core
 
-    def gate_copy(by):
+    def gate_half(ref, half):
+        return ref.at[pl.ds(128 * half, 128), :]
+
+    def gate_copy(by, half):
         return pltpu.make_async_remote_copy(
-            src_ref=gate_own,
-            dst_ref=gate_v.at[slot],
+            src_ref=gate_half(gate_own, half),
+            dst_ref=gate_half(gate_v.at[slot], half),
             send_sem=gate_send.at[by],
-            recv_sem=gate_recv.at[slot, 0],
+            recv_sem=gate_recv.at[slot, half],
             device_id=device(Z, (0, 1, -1)[by], kind),
             device_id_type=MESH,
         )
 
-    def gate_local():
-        return pltpu.make_async_copy(gates, gate_v.at[slot], gate_recv.at[slot, 0])
-
-    def gate_start():
-        stage_gate.wait()
-        gate_copy(1).start()
-        gate_copy(2).start()
+    def gate_start(half):
+        if half == 0:
+            stage_gate.wait()
+        gate_copy(1, half).start()
+        gate_copy(2, half).start()
 
         @pl.when(core == kind)
         def _():
-            gate_local().start()
+            pltpu.make_async_copy(
+                gate_half(gates, half), gate_half(gate_v.at[slot], half), gate_recv.at[slot, half]
+            ).start()
 
         @pl.when(core != kind)
         def _():
-            gate_copy(0).start()
-
-    def gate_half(j, half):
-        return gate_v.at[j, pl.ds(128 * half, 128), :]
+            gate_copy(0, half).start()
 
     def gate_pass(j, half):
+        part = gate_half(gate_v.at[j], half)
         return pltpu.make_async_remote_copy(
-            src_ref=gate_half(j, half),
-            dst_ref=gate_half(j, half),
+            src_ref=part,
+            dst_ref=part,
             send_sem=pass_send.at[j],
             recv_sem=gate_recv.at[j, half],
             device_id=device(Z, 1 - 2 * half, core),
@@ -360,37 +367,29 @@
     def gate_each(act):
         for j in range(HEADS):
             away = (z + 8 - (2 * core + j // 2)) % 4
-            act(j, away)
-
-    def gate_forward(j, away):
-        @pl.when(away == 0)
-        def _():
-            landed(gate_v.at[j], gate_recv.at[j, 0])
-
-        @pl.when(away == 1)
-        def _():
-            landed(gate_v.at[j], gate_recv.at[j, 0])
-            gate_pass(j, 0).start()
-
-        @pl.when(away == 3)
-        def _():
-            landed(gate_v.at[j], gate_recv.at[j, 0])
-            gate_pass(j, 1).start()
-
-    def gate_end(j, away):
-        @pl.when(away == 2)
-        def _():
-            landed(gate_half(j, 0), gate_recv.at[j, 0])
-            landed(gate_half(j, 1), gate_recv.at[j, 1])
-
-    def gate_drain(j, away):
-        @pl.when(away == 1)
-        def _():
-            gate_pass(j, 0).wait_send()
-
-        @pl.when(away == 3)
-        def _():
-            gate_pass(j, 1).wait_send()
+            for half in range(2):
+                act(j, half, away == 1 + 2 * half)
+
+    def gate_forward(wanted):
+        def act(j, half, passed):
+            if half == wanted:
+
+                @pl.when(passed)
+                def _():
+                    landed(gate_half(gate_v.at[j], half), gate_recv.at[j, half])
+                    gate_pass(j, half).start()
+
+        gate_each(act)
+
+    def gate_end(j, half, passed):
+        @pl.when(jnp.logical_not(passed))
+        def _():
+            landed(gate_half(gate_v.at[j], half), gate_recv.at[j, half])
+
+    def gate_drain(j, half, passed):
+        @pl.when(passed)
+        def _():
+            gate_pass(j, half).wait_send()
 
     def norm_rows(i, first):
         rows = pl.ds(pl.multiple_of(i * 16, 16), 16)
@@ -576,13 +575,14 @@
         elif kind == "2s":
             once(("first", group_of(n)), lambda: first_ready(group_of(n)))
             p2_start(n)
-            once("give", give_tokens.start)
         elif kind == "2f":
             p2_pass(n)
         elif kind == "3s":
             p3_start(n)
         elif kind == "3f":
             p3_pass(n)
+        elif kind == "t":
+            give_tokens(n).start()
         elif kind == "h":
             halo_start()
         elif kind == "hf":
@@ -590,14 +590,14 @@
         elif kind == "nh":
             halo_norm()
         elif kind == "g0":
-            gate_start()
+            gate_start(n)
         elif kind == "g1":
-            gate_each(gate_forward)
+            gate_forward(n)
         elif kind == "no":
             once("mine", my_tokens.wait)
             norm(core, n)
         elif kind == "nt":
-            once("theirs", give_tokens.wait_recv)
+            give_tokens(n).wait_recv()
             norm(other, n)
         elif kind == "L1":
             wait(2, n, 1)
@@ -623,7 +623,7 @@
     landed(outs, out_sem)
     landed(ends.at[:, pl.ds(0, 3)], end_send)
     with jax.named_scope("rest"):
-        give_tokens.wait_send()
+        landed(xn.at[pl.ds(HALO, 512), :], tok_sem.at[1])
 
     @pl.when(core == 1)
     def _():
@@ -631,10 +631,10 @@
 
     @pl.when(core != kind)
     def _():
-        gate_copy(0).wait_send()
-
-    gate_copy(1).wait_send()
-    gate_copy(2).wait_send()
+        landed(gate_own, gate_send.at[0])
+
+    landed(gate_own, gate_send.at[1])
+    landed(gate_own, gate_send.at[2])
     gate_each(gate_drain)
     landed(w.at[pl.ds(0, 7), x, y, z], p1_send.at[0])
     landed(w.at[pl.ds(0, 5), pl.ds(0, 3), y, z], p1_send.at[1])
@@ -664,7 +664,7 @@
             pltpu.VMEM((HEADS, ROWS, BW), jnp.float32),
             pltpu.VMEM((HEADS, 512, BW), jnp.bfloat16),
             pltpu.VMEM((HEADS, 4, 2, 8, BW), jnp.float32),
-            dma,
+            dma((3,)),
             dma((3,)),
             dma((3,)),
             dma((3,)),
@@ -673,7 +673,8 @@
             dma((CHUNKS, 2)),
             dma,
             dma((CHUNKS, 2)),
-            dma((3,)),
+            dma((2,)),
+            dma((4,)),
             dma((3,)),
             dma((4,)),
             dma((HEADS, 2)),

time: 87.5 us -> 83.8 us (0.958)
  Pallas kernels: 86 us -> 82.3 us
    pallas_call x1, Pallas kernels: 86 us -> 82.3 us  [shards(): pl.pallas_call(body, name='branch', out_shape=pltpu.VMEM((1, 512, 2048),...]
where the time goes in v4:
time: 83.8 us; the launch traced here: 83.7 us
  Pallas kernels  82.3 us (98%)
  local copies, waits for them, and re-layouts  1.32 us (2%)
    pallas_call x1, Pallas kernels, shards(): pl.pallas_call(body, name='branch', out_shape=pltpu.VMEM((1, 512, 2048),...  82.3 us

profile of v4, /device:TPU:1, one launch (start us, length us, event | category | flops | bytes accessed | tf_op | source)
XLA Modules:
  0.0 83.7 jit_solution(12240211338487461154)
XLA Ops:
  0.0 82.3 %branch.1 = bf16[1,512,2048]{2,1,0:T(8,128)(2,1)S(1)} custom-call(bf16[1,512,4096]{2,1,0:T(8,128)(2,1)} %tokens.1, f32[1,4096]{1,0:T(1,128)} %bitcast.3, bf16[32,2048]{1,0:T(8,128)(2,1)} %lru.1, bf16[32,2048]{1,0:T(8,128)(2,1)} %gelu.1, f32[4,2048]{1,0:T(4,128)} %conv_w.1, f32[1,2048]{1,0:T(1,128)} %bitcast.4, bf16[256,512]{1,0:T(8,128)(2,1)} %gates.1, ...), custom_call_target="tpu_custom_call" | custom-call | tf_op jit(solution)/shard_map/branch/pallas_call | solution.py:650
  82.4 1.3 %copy.11 = bf16[1,512,2048]{2,1,0:T(8,128)(2,1)} copy(bf16[1,512,2048]{2,1,0:T(8,128)(2,1)S(1)} %branch.1) | data formatting | bytes 4194304

commit v5 on v4

--- a/solution.py
+++ b/solution.py
@@ -130,8 +130,8 @@
 
 
 def body(
-    tokens, gain, lru, gelu, conv_w, conv_b, gates, gate_b, decay_p, out,
-    xn, w, stage, gate_own, gate_v, rec, local, cumul, outs, ends,
+    tokens, gain_in, lru, gelu, conv_w_in, conv_b_in, gates, gate_b_in, decay_p_in, out,
+    gain, conv_w, conv_b, gate_b, decay_p, small_sem, xn, w, stage, gate_own, gate_v, rec, local, cumul, outs, ends,
     own_sem, p1_send, p1_recv, pass_recv, pair_recv, p2_send, p2_recv, p3_send, p3_recv,
     tok_sem, tok_recv, halo_sem, gate_send, gate_recv, pass_send, end_send, end_recv, out_sem, out_recv,
 ):
@@ -149,6 +149,17 @@
 
     def group_at(n):
         return [low + count > n for low, count, _ in GROUPS].index(True)
+
+    xn[pl.ds(0, HALO), :] = jnp.zeros((HALO, WIDTH), jnp.bfloat16)
+
+    barrier = pltpu.get_barrier_semaphore()
+    pl.semaphore_signal(barrier, inc=1, device_id=partner, device_id_type=MESH)
+    for dim in (X, Y, Z):
+        for by in (1, 2, 3):
+            for on in range(2):
+                pl.semaphore_signal(
+                    barrier, inc=1, device_id=device(dim, by, on), device_id_type=MESH
+                )
 
     my_part = pl.ds(pl.multiple_of(core * 32, 32), 32)
     own_copies = []
@@ -164,17 +175,20 @@
     for copy in own_copies:
         copy.start()
 
-    xn[pl.ds(0, HALO), :] = jnp.zeros((HALO, WIDTH), jnp.bfloat16)
-
-    barrier = pltpu.get_barrier_semaphore()
-    pl.semaphore_signal(barrier, inc=1, device_id=partner, device_id_type=MESH)
-    for dim in (X, Y, Z):
-        for by in (1, 2, 3):
-            for on in range(2):
-                pl.semaphore_signal(
-                    barrier, inc=1, device_id=device(dim, by, on), device_id_type=MESH
-                )
-
+    small_copies = [
+        pltpu.make_async_copy(src, dst, small_sem.at[i])
+        for i, (src, dst) in enumerate(
+            (
+                (gain_in, gain),
+                (conv_w_in, conv_w),
+                (conv_b_in, conv_b),
+                (gate_b_in, gate_b),
+                (decay_p_in, decay_p),
+            )
+        )
+    ]
+    for copy in small_copies:
+        copy.start()
     my_rows = pl.ds(pl.multiple_of(HALO + core * 512, 16), 512)
     my_tokens = pltpu.make_async_copy(tokens.at[0], xn.at[my_rows, :], tok_sem.at[0])
     my_tokens.start()
@@ -471,8 +485,9 @@
 
         begin = (jnp.ones((8, BW), jnp.float32), jnp.zeros((8, BW), jnp.float32))
         end_a, end_b = lax.fori_loop(0, ROWS // T_ROWS, tile, begin)
-        ends[head, z, 0, :, :] = end_a
-        ends[head, z, 1, :, :] = end_b
+        for row, value in ((0, end_a), (4, end_b)):
+            ends[head, z, row : row + 2, :] = value[0:2, :128]
+            ends[head, z, row + 2 : row + 4, :] = value[0:2, 128:]
 
     def gates_of(head):
         return gate_v[head]
@@ -503,9 +518,16 @@
     def gelu_chunk(head):
         n = GELU_AT[head]
         ends_landed(head)
-        begin = jnp.zeros((8, BW), jnp.float32)
+        begin = jnp.zeros((1, BW), jnp.float32)
         for source in range(3):
-            after = ends[head, source, 0] * begin + ends[head, source, 1]
+            part_a, part_b = (
+                jnp.concatenate(
+                    [ends[head, source, row : row + 1, :], ends[head, source, row + 2 : row + 3, :]],
+                    axis=1,
+                )
+                for row in (0, 4)
+            )
+            after = part_a * begin + part_b
             begin = jnp.where(source < z, after, begin)
         def rows_of(side):
             first = pl.multiple_of(side * 512, 512)
@@ -515,7 +537,7 @@
                 preferred_element_type=jnp.float32,
             )
 
-        start_state = begin[0:1, :]
+        start_state = begin
 
         def part(i, side):
             rows = pl.ds(pl.multiple_of(side * 512 + i * T_ROWS, T_ROWS), T_ROWS)
@@ -595,6 +617,7 @@
             gate_forward(n)
         elif kind == "no":
             once("mine", my_tokens.wait)
+            once("gain", small_copies[0].wait)
             norm(core, n)
         elif kind == "nt":
             give_tokens(n).wait_recv()
@@ -605,6 +628,8 @@
         elif kind == "L2":
             if n == 0:
                 gate_each(gate_end)
+                for copy in small_copies[1:]:
+                    copy.wait()
             lru_tiles(SEQUENCE[n][1])
             for by in range(1, 4):
                 end_copy(SEQUENCE[n][1], by).start()
@@ -651,9 +676,15 @@
         body,
         name="branch",
         out_shape=pltpu.VMEM((1, 512, 2048), jnp.bfloat16),
-        in_specs=[hbm, vmem, hbm, hbm, vmem, vmem, hbm, vmem, vmem],
+        in_specs=[hbm] * 9,
         out_specs=vmem,
         scratch_shapes=[
+            pltpu.VMEM((1, WIDTH), jnp.float32),
+            pltpu.VMEM((4, 2 * HEADS * BW), jnp.float32),
+            pltpu.VMEM((1, 2 * HEADS * BW), jnp.float32),
+            pltpu.VMEM((2, 2 * HEADS * BW), jnp.float32),
+            pltpu.VMEM((1, 2 * HEADS * BW), jnp.float32),
+            dma((5,)),
             pltpu.VMEM((HALO + ROWS, WIDTH), jnp.bfloat16),
             pltpu.VMEM((CHUNKS, 4, 4, 4, 64, BW), jnp.bfloat16),
             pltpu.VMEM((CHUNKS, 32, BW), jnp.bfloat16),
@@ -663,7 +694,7 @@
             pltpu.VMEM((HEADS, ROWS, BW), jnp.float32),
             pltpu.VMEM((HEADS, ROWS, BW), jnp.float32),
             pltpu.VMEM((HEADS, 512, BW), jnp.bfloat16),
-            pltpu.VMEM((HEADS, 4, 2, 8, BW), jnp.float32),
+            pltpu.VMEM((HEADS, 4, 8, 128), jnp.float32),
             dma((3,)),
             dma((3,)),
             dma((3,)),

time: 83.8 us -> 83 us (level)
  no operation moved by 1% of the time
where the time goes in v5:
time: 83 us; the launch traced here: 82.9 us
  Pallas kernels  81.6 us (98%)
  local copies, waits for them, and re-layouts  1.32 us (2%)
    pallas_call x1, Pallas kernels, shards(): pl.pallas_call(body, name='branch', out_shape=pltpu.VMEM((1, 512, 2048),...  81.6 us

profile of v5, /device:TPU:1, one launch (start us, length us, event | category | flops | bytes accessed | tf_op | source)
XLA Modules:
  0.0 82.9 jit_solution(2120705178170017492)
XLA Ops:
  0.0 81.6 %branch.1 = bf16[1,512,2048]{2,1,0:T(8,128)(2,1)S(1)} custom-call(bf16[1,512,4096]{2,1,0:T(8,128)(2,1)} %tokens.1, f32[1,4096]{1,0:T(1,128)} %bitcast.3, bf16[32,2048]{1,0:T(8,128)(2,1)} %lru.1, bf16[32,2048]{1,0:T(8,128)(2,1)} %gelu.1, f32[4,2048]{1,0:T(4,128)} %conv_w_in.1, f32[1,2048]{1,0:T(1,128)} %bitcast.4, bf16[256,512]{1,0:T(8,128)(2,1)} %gates.1, ...), custom_call_target="tpu_custom_call" | custom-call | tf_op jit(solution)/shard_map/branch/pallas_call | solution.py:675
  81.6 1.3 %copy.11 = bf16[1,512,2048]{2,1,0:T(8,128)(2,1)} copy(bf16[1,512,2048]{2,1,0:T(8,128)(2,1)S(1)} %branch.1) | data formatting | bytes 4194304

commit v6 on v5

--- a/solution.py
+++ b/solution.py
@@ -25,7 +25,7 @@
 GELU_AT = tuple(SEQUENCE.index((1, head)) for head in range(HEADS))
 GROUPS = ((0, 2, USUAL), (2, 4, USUAL), (6, 2, LATE))
 PLAN = (
-    ("t", 1), ("g0", 0), ("1p", 2), ("2s", 0), ("no", 0), ("2s", 1), ("1p", 6), ("h",), ("2s", 3), ("2s", 2),
+    ("g0", 0), ("1p", 2), ("2s", 0), ("no", 0), ("t", 1), ("2s", 1), ("1p", 6), ("h",), ("2s", 3), ("2s", 2),
     ("2f", 0), ("t", 0), ("2s", 6), ("2s", 5), ("no", 1), ("2f", 1), ("2f", 3), ("2f", 2), ("hf",), ("2s", 4),
     ("3s", 0), ("t", 2), ("no", 2), ("no", 3), ("3s", 1), ("g0", 1), ("2f", 4), ("3s", 2), ("nt", 0), ("3f", 0),
     ("t", 3), ("g1", 1), ("g1", 0), ("3s", 3), ("2f", 5), ("2f", 6), ("3f", 1), ("3f", 2), ("nt", 1), ("3s", 4),

time: 83 us -> 83 us (level)
  no operation moved by 1% of the time
where the time goes in v6:
time: 83 us; the launch traced here: 82.9 us
  Pallas kernels  81.6 us (98%)
  local copies, waits for them, and re-layouts  1.32 us (2%)
    pallas_call x1, Pallas kernels, shards(): pl.pallas_call(body, name='branch', out_shape=pltpu.VMEM((1, 512, 2048),...  81.6 us

profile of v6, /device:TPU:1, one launch (start us, length us, event | category | flops | bytes accessed | tf_op | source)
XLA Modules:
  0.0 82.9 jit_solution(7774178634668449769)
XLA Ops:
  0.0 81.6 %branch.1 = bf16[1,512,2048]{2,1,0:T(8,128)(2,1)S(1)} custom-call(bf16[1,512,4096]{2,1,0:T(8,128)(2,1)} %tokens.1, f32[1,4096]{1,0:T(1,128)} %bitcast.3, bf16[32,2048]{1,0:T(8,128)(2,1)} %lru.1, bf16[32,2048]{1,0:T(8,128)(2,1)} %gelu.1, f32[4,2048]{1,0:T(4,128)} %conv_w_in.1, f32[1,2048]{1,0:T(1,128)} %bitcast.4, bf16[256,512]{1,0:T(8,128)(2,1)} %gates.1, ...), custom_call_target="tpu_custom_call" | custom-call | tf_op jit(solution)/shard_map/branch/pallas_call | solution.py:675
  81.6 1.3 %copy.11 = bf16[1,512,2048]{2,1,0:T(8,128)(2,1)} copy(bf16[1,512,2048]{2,1,0:T(8,128)(2,1)S(1)} %branch.1) | data formatting | bytes 4194304
